TPU v7x, 16 devices: a whole 2x2x2 slice. The times are simulated.
16 devices in a mesh: replica: 2 (over z), data: 8 (over y, x, core).
Axes of the slice: x: 2, y: 2, z: 2, core: 2. Of those that a mesh axis runs over, the one named last changes fastest.
Arguments:
- x_seq: bfloat16 [512, 16, 1024], P(('replica', 'data'))
- dy_seq: float32 [512, 16, 1024], P(('replica', 'data'))
- w_stack: bfloat16 [4, 2048, 4096], replicated
- b_stack: float32 [4, 4096], replicated
Outputs:
- output 1: float32 [4, 2048, 4096], replicated
- output 2: float32 [4, 4096], replicated
- output 3: float32 [512, 16, 1024], P(('replica', 'data'))
All inputs are finite; a program needn't handle non-finite values.
Results may differ from a plain program's by a relative error of at most 0.0150577.
Values are sent between devices in bfloat16 or wider.
A program may use at most 1 GiB of HBM per device.

v0:
```python
import jax
import jax.numpy as jnp
from jax import lax
from jax.sharding import PartitionSpec as P


def layer_forward(u_seq, w_layer, b_layer):
    hidden = u_seq.shape[-1]
    batch_rows = u_seq.shape[1]
    w_rec = w_layer[hidden:]
    in_proj = jnp.einsum('tbh,hg->tbg', u_seq, w_layer[:hidden], preferred_element_type=jnp.float32) + b_layer

    def time_step(carry_state, z_in):
        h_prev, c_prev = carry_state
        z_all = z_in + jnp.dot(h_prev, w_rec, preferred_element_type=jnp.float32)
        z_i, z_f, z_g, z_o = jnp.split(z_all, 4, axis=-1)
        gate_i = jax.nn.sigmoid(z_i)
        gate_f = jax.nn.sigmoid(z_f)
        gate_g = jnp.tanh(z_g)
        gate_o = jax.nn.sigmoid(z_o)
        c_new = gate_f * c_prev + gate_i * gate_g
        tanh_c = jnp.tanh(c_new)
        h_new = (gate_o * tanh_c).astype(jnp.bfloat16)
        return (h_new, c_new), (h_new, c_new, tanh_c, gate_i, gate_f, gate_g, gate_o)

    init_state = (jnp.zeros((batch_rows, hidden), jnp.bfloat16), jnp.zeros((batch_rows, hidden), jnp.float32))
    return lax.scan(time_step, init_state, in_proj)[1]


def layer_backward(u_seq, w_layer, saved_acts, dh_seq):
    hidden = u_seq.shape[-1]
    h_seq, c_seq, tanh_seq, i_seq, f_seq, g_seq, o_seq = saved_acts
    h_prev_seq = jnp.concatenate([jnp.zeros_like(h_seq[:1]), h_seq[:-1]], axis=0)
    c_prev_seq = jnp.concatenate([jnp.zeros_like(c_seq[:1]), c_seq[:-1]], axis=0)
    w_rec = w_layer[hidden:]

    def time_step(carry_state, step_in):
        dh_rec, dc_next = carry_state
        dh_out, c_prev, tanh_c, gate_i, gate_f, gate_g, gate_o = step_in
        dh_tot = dh_out + dh_rec
        dc_cur = dc_next + dh_tot * gate_o * (1.0 - tanh_c * tanh_c)
        dz_all = jnp.concatenate([dc_cur * gate_g * gate_i * (1.0 - gate_i), dc_cur * c_prev * gate_f * (1.0 - gate_f), dc_cur * gate_i * (1.0 - gate_g * gate_g), dh_tot * tanh_c * gate_o * (1.0 - gate_o)], axis=-1)
        dz_low = dz_all.astype(jnp.bfloat16)
        dh_prev = jnp.einsum('bg,hg->bh', dz_low, w_rec, preferred_element_type=jnp.float32)
        return (dh_prev, dc_cur * gate_f), (dz_low, jnp.sum(dz_all, axis=0))

    init_state = (jnp.zeros_like(dh_seq[0]), jnp.zeros_like(dh_seq[0]))
    dz_seq, db_steps = lax.scan(time_step, init_state, (dh_seq, c_prev_seq, tanh_seq, i_seq, f_seq, g_seq, o_seq), reverse=True)[1]
    dx_seq = jnp.einsum('tbg,hg->tbh', dz_seq, w_layer[:hidden], preferred_element_type=jnp.float32)
    dw_in = jnp.einsum('tbh,tbg->hg', u_seq, dz_seq, preferred_element_type=jnp.float32)
    dw_rec = jnp.einsum('tbh,tbg->hg', h_prev_seq, dz_seq, preferred_element_type=jnp.float32)
    return jnp.concatenate([dw_in, dw_rec], axis=0), jnp.sum(db_steps, axis=0), dx_seq


def reduce_weights(dw_part):
    part_low = dw_part.astype(jnp.bfloat16)
    shard_sum = lax.psum_scatter(part_low, 'data', scatter_dimension=0, tiled=True)
    shard_sum = lax.psum(shard_sum, 'replica')
    return lax.all_gather(shard_sum, 'data', axis=0, tiled=True).astype(jnp.float32)


def solution(mesh):
    batch_axes = ('replica', 'data')

    def local_grads(x_loc, dy_loc, w_stack, b_stack):
        layers = w_stack.shape[0]
        u_seq = jnp.swapaxes(x_loc, 0, 1)
        layer_inputs = []
        layer_saved = []
        for layer_idx in range(layers):
            saved_acts = layer_forward(u_seq, w_stack[layer_idx], b_stack[layer_idx])
            layer_inputs.append(u_seq)
            layer_saved.append(saved_acts)
            u_seq = saved_acts[0]
        dh_seq = jnp.swapaxes(dy_loc, 0, 1)
        dw_list = []
        db_list = []
        for layer_idx in reversed(range(layers)):
            dw_part, db_part, dh_seq = layer_backward(layer_inputs[layer_idx], w_stack[layer_idx], layer_saved[layer_idx], dh_seq)
            dw_list.append(reduce_weights(dw_part))
            db_list.append(lax.psum(db_part.astype(jnp.bfloat16), batch_axes).astype(jnp.float32))
        return jnp.stack(dw_list[::-1]), jnp.stack(db_list[::-1]), jnp.swapaxes(dh_seq, 0, 1)

    return jax.shard_map(local_grads, mesh=mesh, in_specs=(P(batch_axes), P(batch_axes), P(), P()), out_specs=(P(), P(), P(batch_axes)), check_vma=False)
```

profile of v0, /device:TPU:0, one launch (start us, length us, event | category | flops | bytes accessed | tf_op | source)
XLA Modules:
  0.0 2005.8 jit_solution(16912641742901432732)
XLA Ops:
  12.5 23.1 %slice_bitcast_fusion = (bf16[1024,4096]{1,0:T(8,128)(2,1)}, bf16[1024,4096]{1,0:T(8,128)(2,1)}, bf16[1024,4096]{1,0:T(8,128)(2,1)}, bf16[1024,4096]{1,0:T(8,128)(2,1)}) fusion(bf16[4,2048,4096]{2,1,0:T(8,128)(2,1)} %param.22), kind=kLoop, calls=%fused_computation.273 | loop fusion | bytes 67108864 | tf_op jit(solution)/shard_map/slice | solution.py:10
  35.6 10.3 fusion.137
  55.3 105.7 %while.192 = (s32[]{:T(128)}, bf16[32,1024]{1,0:T(8,128)(2,1)S(1)}, f32[32,1024]{1,0:T(8,128)S(1)}, bf16[16,32,1024]{2,1,0:T(8,128)(2,1)}, f32[16,32,1024]{2,1,0...) while((s32[]{:T(128)}, bf16[32,1024]{1,0:T(8,128)(2,1)S(1)}, ...), condition=%wide.region_1.2_spmd.clone, body=%wide.region_0.1_spmd.clone.sunk | while | flops 269189120 | bytes 11600040 | solution.py:27
  161.0 12.4 fusion.140
  182.8 106.1 %while.193 = (s32[]{:T(128)}, bf16[32,1024]{1,0:T(8,128)(2,1)S(1)}, f32[32,1024]{1,0:T(8,128)S(1)}, bf16[16,32,1024]{2,1,0:T(8,128)(2,1)}, f32[16,32,1024]{2,1,0...) while((s32[]{:T(128)}, bf16[32,1024]{1,0:T(8,128)(2,1)S(1)}, ...), condition=%wide.region_3.4_spmd.clone, body=%wide.region_2.3_spmd.clone.sunk | while | flops 269189120 | bytes 11600040 | solution.py:27
  288.8 12.4 fusion.143
  310.6 105.7 %while.194 = (s32[]{:T(128)}, bf16[32,1024]{1,0:T(8,128)(2,1)S(1)}, f32[32,1024]{1,0:T(8,128)S(1)}, bf16[16,32,1024]{2,1,0:T(8,128)(2,1)}, f32[16,32,1024]{2,1,0...) while((s32[]{:T(128)}, bf16[32,1024]{1,0:T(8,128)(2,1)S(1)}, ...), condition=%wide.region_5.6_spmd.clone, body=%wide.region_4.5_spmd.clone.sunk | while | flops 269189120 | bytes 11600040 | solution.py:27
  416.3 12.4 fusion.146
  437.9 106.0 %while.195 = (s32[]{:T(128)}, bf16[32,1024]{1,0:T(8,128)(2,1)S(1)}, f32[32,1024]{1,0:T(8,128)S(1)}, bf16[16,32,1024]{2,1,0:T(8,128)(2,1)}, f32[16,32,1024]{2,1,0...) while((s32[]{:T(128)}, bf16[32,1024]{1,0:T(8,128)(2,1)S(1)}, ...), condition=%wide.region_7.8_spmd.clone, body=%wide.region_6.7_spmd.clone.sunk | while | flops 269189120 | bytes 11600040 | solution.py:27
  547.1 152.0 %while.196 = (s32[]{:T(128)}, f32[32,1024]{1,0:T(8,128)S(1)}, f32[32,1024]{1,0:T(8,128)S(1)}, bf16[16,32,4096]{2,1,0:T(8,128)(2,1)}, f32[16,4096]{1,0:T(8,128)S(...) while((s32[]{:T(128)}, f32[32,1024]{1,0:T(8,128)S(1)}, ...), condition=%wide.region_10.11_spmd.clone, body=%wide.region_8.10_spmd.clone.sunk | while | flops 271970304 | bytes 12763331 | solution.py:48
  549.7 6.0 fusion.243
  568.7 6.0 fusion.243
  578.1 6.0 fusion.243
  587.6 6.0 fusion.243
  606.6 6.0 fusion.243
  616.1 6.0 fusion.243
  635.0 6.0 fusion.243
  663.5 6.0 fusion.243
  673.0 6.0 fusion.243
  682.4 6.0 fusion.243
  699.0 7.2 bitcast_convert_fusion.1
  711.1 7.0 pad_maximum_fusion.7
  718.2 10.6 fusion.112
  731.8 152.1 %while.197 = (s32[]{:T(128)}, f32[32,1024]{1,0:T(8,128)S(1)}, f32[32,1024]{1,0:T(8,128)S(1)}, bf16[16,32,4096]{2,1,0:T(8,128)(2,1)}, f32[16,4096]{1,0:T(8,128)S(...) while((s32[]{:T(128)}, f32[32,1024]{1,0:T(8,128)S(1)}, ...), condition=%wide.region_13.14_spmd.clone, body=%wide.region_11.13_spmd.clone.sunk | while | flops 271970304 | bytes 12763331 | solution.py:48
  734.6 6.0 fusion.247
  744.1 6.0 fusion.247
  763.1 6.0 fusion.247
  801.0 6.0 fusion.247
  820.0 6.0 fusion.247
  829.4 6.0 fusion.247
  848.4 6.0 fusion.247
  876.9 6.0 fusion.247
  883.9 7.2 bitcast_convert_fusion.2
  896.0 7.2 pad_maximum_fusion.6
  903.5 10.6 fusion.116
  917.1 151.7 %while.198 = (s32[]{:T(128)}, f32[32,1024]{1,0:T(8,128)S(1)}, f32[32,1024]{1,0:T(8,128)S(1)}, bf16[16,32,4096]{2,1,0:T(8,128)(2,1)}, f32[16,4096]{1,0:T(8,128)S(...) while((s32[]{:T(128)}, f32[32,1024]{1,0:T(8,128)S(1)}, ...), condition=%wide.region_16.17_spmd.clone, body=%wide.region_14.16_spmd.clone.sunk | while | flops 271970304 | bytes 12763331 | solution.py:48
  929.0 6.0 fusion.251
  947.9 6.0 fusion.251
  976.4 6.0 fusion.251
  995.4 6.0 fusion.251
  1042.8 6.0 fusion.251
  1061.7 6.0 fusion.251
  1068.8 7.2 bitcast_convert_fusion.4
  1080.9 7.4 pad_maximum_fusion.5
  1088.6 10.6 fusion.120
  1102.2 151.8 %while.199 = (s32[]{:T(128)}, f32[32,1024]{1,0:T(8,128)S(1)}, f32[32,1024]{1,0:T(8,128)S(1)}, bf16[16,32,4096]{2,1,0:T(8,128)(2,1)}, f32[16,4096]{1,0:T(8,128)S(...) while((s32[]{:T(128)}, f32[32,1024]{1,0:T(8,128)S(1)}, ...), condition=%wide.region_19.20_spmd.clone, body=%wide.region_17.19_spmd.clone.sunk | while | flops 271970304 | bytes 12763331 | solution.py:48
  1114.1 6.0 fusion.255
  1123.5 6.0 fusion.255
  1133.0 6.0 fusion.255
  1152.0 6.0 fusion.255
  1161.5 6.0 fusion.255
  1180.4 6.0 fusion.255
  1218.4 6.0 fusion.255
  1254.0 7.3 fusion.136
  1266.2 7.1 pad_maximum_fusion.4
  1273.4 112.5 %reduce-scatter.5.cloned.1.call-done = bf16[256,4096]{1,0:T(8,128)(2,1)} async-done(((bf16[2048,4096]{1,0:T(8,128)(2,1)}), bf16[256,4096]{1,0:T(8,128)(2,1)}) %reduce-scatter.5.cloned.1.call-update) | async-done | bytes 2097168 | tf_op jit(solution)/shard_map/reduce_scatter | solution.py:57
  1386.0 196.6 %all-reduce.12.cloned.1.call-done = (bf16[256,4096]{1,0:T(8,128)(2,1)}, bf16[256,4096]{1,0:T(8,128)(2,1)}, bf16[256,4096]{1,0:T(8,128)(2,1)}, bf16[256,4096]{1,0:T(8,128)(2,1)}) async-done(((bf16[256,4096]{1,0:T(8,128)(2,1)}, bf16[256,4096]{1,0:T(8,128)(2,1)}, bf16[256,4096]{1,0:T(8,128)(2,1)}, bf16[256,4096]{1,0:T(8,128)(2,1)}), (bf16[256,4096]{1,0:T(8,128)(2,1)}, bf16[256,4096]{1,0:T(8,128)(2,1)}, ...) | async-done | bytes 8388624 | tf_op jit(solution)/shard_map/psum | solution.py:58
  1585.2 8.5 fusion.149
  1596.3 33.6 %all-reduce.8 = (bf16[1,4096]{1,0:T(2,128)(2,1)S(1)}, bf16[1,4096]{1,0:T(2,128)(2,1)S(1)}, bf16[1,4096]{1,0:T(2,128)(2,1)S(1)}, bf16[1,4096]{1,0:T(2,128)(2,1)S(1)}) all-reduce(bf16[1,4096]{1,0:T(2,128)(2,1)S(1)} %stack.53, bf16[1,4096]{1,0:T(2,128)(2,1)S(1)} %stack.52, ...), channel_id=1, replica_groups=mesh['replica'=2,'data'=8] {'replica','data'}, use_global_device_ids=true, to_apply=%region_35.36 | all-reduce | flops 16384 | bytes 65536 | tf_op jit(solution)/shard_map/psum | solution.py:81
  1630.5 41.5 %all-gather.11.cloned.1.call-done = bf16[2048,4096]{1,0:T(8,128)(2,1)} async-done(((bf16[256,4096]{1,0:T(8,128)(2,1)}), bf16[2048,4096]{1,0:T(8,128)(2,1)}) %all-gather.11.cloned.1.call-update) | async-done | bytes 16777232 | tf_op jit(solution)/shard_map/all_gather | solution.py:59
  1672.1 87.8 %all-gather.9.cloned.1.call-done = bf16[2048,4096]{1,0:T(8,128)(2,1)} async-done(((bf16[256,4096]{1,0:T(8,128)(2,1)}), bf16[2048,4096]{1,0:T(8,128)(2,1)}) %all-gather.9.cloned.1.call-update) | async-done | bytes 16777232 | tf_op jit(solution)/shard_map/all_gather | solution.py:59
  1759.8 87.8 %all-gather.7.cloned.1.call-done = bf16[2048,4096]{1,0:T(8,128)(2,1)} async-done(((bf16[256,4096]{1,0:T(8,128)(2,1)}), bf16[2048,4096]{1,0:T(8,128)(2,1)}) %all-gather.7.cloned.1.call-update) | async-done | bytes 16777232 | tf_op jit(solution)/shard_map/all_gather | solution.py:59
  1847.6 87.8 %all-gather.5.cloned.1.call-done = bf16[2048,4096]{1,0:T(8,128)(2,1)} async-done(((bf16[256,4096]{1,0:T(8,128)(2,1)}), bf16[2048,4096]{1,0:T(8,128)(2,1)}) %all-gather.5.cloned.1.call-update) | async-done | bytes 16777232 | tf_op jit(solution)/shard_map/all_gather | solution.py:59
  1935.3 63.5 %maximum_convert_fusion = f32[4,2048,4096]{2,1,0:T(8,128)} fusion(bf16[1,2048,4096]{2,1,0:T(8,128)(2,1)} %bitcast.554, bf16[1,2048,4096]{2,1,0:T(8,128)(2,1)} %bitcast.555, bf16[1,2048,4096]{2,1,0:T(8,128)(2,1)} %bitcast.556, bf16[1,2048,4096]{2,1,0:T(8,128)(2,1)} %bitcast.557), kind=kLoop, calls=%fused_computation.244 | loop fusion | flops 134217728 | bytes 201326592 | tf_op jit(solution)/shard_map/stack | solution.py:82
  (750 shorter events, 922.8 us)
Async XLA Ops:
  7.2 1266.2 %reduce-scatter.11.cloned.1.call-start = ((), (), s32[]{:S(2)}) async-start(), calls=%async_computation.10 | async-start | bytes 18874368 | tf_op jit(solution)/shard_map/reduce_scatter | solution.py:57
  12.5 23.1 %copy-start.21 = (bf16[32,16,1024]{2,1,0:T(8,128)(2,1)S(1)}, bf16[32,16,1024]{2,1,0:T(8,128)(2,1)}, u32[]{:S(2)}) copy-start(bf16[32,16,1024]{2,1,0:T(8,128)(2,1)} %param.20) | copy-start | bytes 3145732
  161.0 12.4 copy-start
  288.8 12.4 copy-start.2
  416.3 12.4 copy-start.4
  544.5 2.5 copy-start.10
  699.0 7.2 copy-start.15
  699.0 7.2 copy-start.7
  699.0 7.3 copy-start.14
  718.2 555.2 %reduce-scatter.9.cloned.1.call-start = ((), (), s32[]{:S(2)}) async-start(), calls=%async_computation.8 | async-start | bytes 18874368 | tf_op jit(solution)/shard_map/reduce_scatter | solution.py:57
  718.2 10.6 copy-start.5
  883.9 7.2 copy-start.17
  883.9 7.2 copy-start.8
  883.9 7.2 copy-start.13
  903.3 370.2 %reduce-scatter.7.cloned.1.call-start = ((), (), s32[]{:S(2)}) async-start(), calls=%async_computation.6 | async-start | bytes 18874368 | tf_op jit(solution)/shard_map/reduce_scatter | solution.py:57
  903.5 10.6 copy-start.3
  1068.8 7.2 copy-start.19
  1068.8 7.2 copy-start.9
  1068.8 7.2 copy-start.11
  1088.3 297.7 %reduce-scatter.5.cloned.1.call-start = ((), (), s32[]{:S(2)}) async-start(), calls=%async_computation.4 | async-start | bytes 18874368 | tf_op jit(solution)/shard_map/reduce_scatter | solution.py:57
  1088.6 10.6 copy-start.1
  1253.9 7.4 copy-start.6
  1253.9 7.4 copy-start.12
  1273.3 309.3 %all-reduce.12.cloned.1.call-start = ((), (), s32[]{:S(2)}) async-start(), calls=%async_computation.12 | async-start | bytes 16777216 | tf_op jit(solution)/shard_map/psum | solution.py:58
  1386.0 286.1 %all-gather.11.cloned.1.call-start = ((), (), s32[]{:S(2)}) async-start(), calls=%async_computation.11 | async-start | bytes 18874368 | tf_op jit(solution)/shard_map/all_gather | solution.py:59
  1582.7 177.1 %all-gather.9.cloned.1.call-start = ((), (), s32[]{:S(2)}) async-start(), calls=%async_computation.9 | async-start | bytes 18874368 | tf_op jit(solution)/shard_map/all_gather | solution.py:59
  1583.4 264.2 %all-gather.7.cloned.1.call-start = ((), (), s32[]{:S(2)}) async-start(), calls=%async_computation.7 | async-start | bytes 18874368 | tf_op jit(solution)/shard_map/all_gather | solution.py:59
  1583.5 1.4 copy-start.16
  1583.5 1.5 copy-start.18
  1583.5 1.6 copy-start.20
  1584.2 351.2 %all-gather.5.cloned.1.call-start = ((), (), s32[]{:S(2)}) async-start(), calls=%async_computation.5 | async-start | bytes 18874368 | tf_op jit(solution)/shard_map/all_gather | solution.py:59
Sparse Core Ops, SparseCore 0:
  718.3 112.4 reduce-scatter.10
  903.4 112.4 reduce-scatter.8
  1088.4 112.5 reduce-scatter.6
  1273.4 112.4 reduce-scatter.4
  1388.6 194.0 all-reduce.11
  1584.4 87.6 all-gather.10
  1673.9 85.8 all-gather.8
  1761.7 85.8 all-gather.6
  1849.4 85.8 all-gather.4
where the time goes:
time: 2020 us; the launch traced here: 2010 us
  matrix products  835 us (41%)
  waiting for transfers between devices  616 us (30%)
  other arithmetic  395 us (20%)
  local copies, waits for them, and re-layouts  106 us (5%)
  blocking collectives  33.6 us (2%)
    dot_general x64, matrix products, time_step(): jnp.einsum('bg,hg->bh', dz_low, w_rec, preferred_element_type=jnp.float32)  381 us
    dot_general x64, matrix products, time_step(): z_all = z_in + jnp.dot(h_prev, w_rec, preferred_element_type=jnp.float32)  318 us
    all_gather x4, waiting for transfers between devices, reduce_weights(): lax.all_gather(shard_sum, 'data', axis=0, tiled=True).astype(jnp.float32)  305 us
    psum x1, waiting for transfers between devices, reduce_weights(): shard_sum = lax.psum(shard_sum, 'replica')  197 us
    concatenate x128, other arithmetic, time_step(): jnp.concatenate([dc_cur * gate_g * gate_i * (1.0 - gate_i), dc_cur * c_pr...  150 us
    reduce_scatter x4, waiting for transfers between devices, reduce_weights(): lax.psum_scatter(part_low, 'data', scatter_dimension=0, tiled=True)  113 us
    dynamic_update_slice x128, other arithmetic, layer_forward(): return lax.scan(time_step, init_state, in_proj)[1]  103 us
    another operation x1, other arithmetic, local_grads(): jnp.stack(dw_list[::-1])  63.5 us
  transfers between devices with their start and end apart: 9, of which 6 were waited for; matrix products, arithmetic and copies ran while one was open for 28% of the time, Pallas kernels for 0%

commit v1 on v0

v1 whole, which is shorter than its diff:
```python
import functools

import jax
import jax.numpy as jnp
from jax import lax
from jax.experimental import pallas as pl
from jax.experimental.pallas import tpu as pltpu
from jax.sharding import PartitionSpec as P

VMEM_MAX = 67043328
BLK = 256


def sigmoid(z):
    return 0.5 * jnp.tanh(0.5 * z) + 0.5


def forward_kernel(rows, steps, hidden, x_ref, w_ref, b_ref, h_ref, gates_ref, c_ref, u_ref):
    @pl.when(pl.program_id(0) == 0)
    def _():
        u_ref[...] = x_ref[...]

    h_ref[0, :rows, :] = jnp.zeros((rows, hidden), jnp.bfloat16)
    c_ref[0, :rows, :] = jnp.zeros((rows, hidden), jnp.float32)

    @pl.loop(0, 4 * hidden // BLK)
    def _(n):
        cols = pl.ds(pl.multiple_of(n * BLK, BLK), BLK)
        part = jnp.dot(u_ref[...], w_ref[0, :hidden, cols], preferred_element_type=jnp.float32)
        gates_ref[0, :, cols] = part + b_ref[0, :, cols]

    @pl.loop(0, steps)
    def _(t):
        now = pl.ds(pl.multiple_of(t * rows, rows), rows)
        later = pl.ds(pl.multiple_of(t * rows + rows, rows), rows)
        h_prev = h_ref[0, now, :]
        for j in range(hidden // BLK):
            cols = [pl.ds(k * hidden + j * BLK, BLK) for k in range(4)]
            z = [
                gates_ref[0, now, col] + jnp.dot(h_prev, w_ref[0, hidden:, col], preferred_element_type=jnp.float32)
                for col in cols
            ]
            act = [sigmoid(z[0]), sigmoid(z[1]), jnp.tanh(z[2]), sigmoid(z[3])]
            for col, value in zip(cols, act):
                gates_ref[0, now, col] = value
            part = pl.ds(j * BLK, BLK)
            c_new = act[1] * c_ref[0, now, part] + act[0] * act[2]
            c_ref[0, later, part] = c_new
            h_ref[0, later, part] = (act[3] * jnp.tanh(c_new)).astype(jnp.bfloat16)

    u_ref[...] = h_ref[0, rows:, :]


def forward(x_rows, w_stack, b_stack, rows):
    layers, _, width = w_stack.shape
    hidden = width // 4
    total = x_rows.shape[0]
    steps = total // rows
    return pl.pallas_call(
        functools.partial(forward_kernel, rows, steps, hidden),
        grid=(layers,),
        in_specs=[
            pl.BlockSpec((total, hidden), lambda l: (0, 0)),
            pl.BlockSpec((1, 2 * hidden, width), lambda l: (l, 0, 0)),
            pl.BlockSpec((1, 1, width), lambda l: (l, 0, 0)),
        ],
        out_specs=[
            pl.BlockSpec((1, total + rows, hidden), lambda l: (l, 0, 0)),
            pl.BlockSpec((1, total, width), lambda l: (l, 0, 0)),
            pl.BlockSpec((1, total + rows, hidden), lambda l: (l, 0, 0)),
        ],
        out_shape=[
            jax.ShapeDtypeStruct((layers, total + rows, hidden), jnp.bfloat16),
            jax.ShapeDtypeStruct((layers, total, width), jnp.float32),
            jax.ShapeDtypeStruct((layers, total + rows, hidden), jnp.float32),
        ],
        scratch_shapes=[pltpu.VMEM((total, hidden), jnp.bfloat16)],
        compiler_params=pltpu.CompilerParams(vmem_limit_bytes=VMEM_MAX),
        cost_estimate=pl.CostEstimate(
            flops=2 * layers * total * 2 * hidden * width,
            bytes_accessed=2 * layers * hidden * width + 5 * 4 * layers * total * hidden,
            transcendentals=0,
        ),
        name="lstm_forward",
    )(x_rows, w_stack, b_stack.reshape(layers, 1, width))


def backward_kernel(rows, steps, hidden, e_ref, w_ref, gates_ref, c_ref, dz_ref, db_ref, wt_ref, r_ref, dc_ref):
    blocks = hidden // BLK

    @pl.loop(0, blocks)
    def _(j):
        for k in range(4):
            cols = pl.ds(pl.multiple_of(k * hidden + j * BLK, BLK), BLK)
            place = pl.ds(pl.multiple_of(j * 4 * BLK + k * BLK, BLK), BLK)
            wt_ref[place, :] = w_ref[0, :, cols].T

    r_ref[...] = jnp.zeros_like(r_ref)
    dc_ref[...] = jnp.zeros_like(dc_ref)
    db_ref[...] = jnp.zeros_like(db_ref)

    @pl.loop(0, steps)
    def _(s):
        t = steps - 1 - s
        now = pl.ds(pl.multiple_of(t * rows, rows), rows)
        later = pl.ds(pl.multiple_of(t * rows + rows, rows), rows)
        total = None
        for j in range(blocks):
            part = pl.ds(j * BLK, BLK)
            cols = [pl.ds(k * hidden + j * BLK, BLK) for k in range(4)]
            gate_i, gate_f, gate_g, gate_o = [gates_ref[0, now, col] for col in cols]
            tanh_c = jnp.tanh(c_ref[0, later, part])
            dh = e_ref[now, part] + r_ref[:, part]
            dc = dc_ref[:, part] + dh * gate_o * (1.0 - tanh_c * tanh_c)
            dz = [
                dc * gate_g * gate_i * (1.0 - gate_i),
                dc * c_ref[0, now, part] * gate_f * (1.0 - gate_f),
                dc * gate_i * (1.0 - gate_g * gate_g),
                dh * tanh_c * gate_o * (1.0 - gate_o),
            ]
            dc_ref[:, part] = dc * gate_f
            low = []
            for col, value in zip(cols, dz):
                low.append(value.astype(jnp.bfloat16))
                dz_ref[now, col] = low[-1]
                db_ref[:, col] += jnp.sum(value.reshape(rows // 8, 8, BLK), axis=0)
            back = jnp.dot(
                jnp.concatenate(low, axis=1),
                wt_ref[j * 4 * BLK : (j + 1) * 4 * BLK, :],
                preferred_element_type=jnp.float32,
            )
            total = back if total is None else total + back
        r_ref[...] = total


def backward(layer, e_rows, w_stack, gates, c_all, rows):
    _, _, width = w_stack.shape
    hidden = width // 4
    total = e_rows.shape[0]
    steps = total // rows
    return pl.pallas_call(
        functools.partial(backward_kernel, rows, steps, hidden),
        grid=(1,),
        in_specs=[
            pl.BlockSpec((total, hidden), lambda i: (0, 0), pipeline_mode=pl.Buffered(1)),
            pl.BlockSpec((1, hidden, width), lambda i: (layer, 1, 0), pipeline_mode=pl.Buffered(1)),
            pl.BlockSpec((1, total, width), lambda i: (layer, 0, 0), pipeline_mode=pl.Buffered(1)),
            pl.BlockSpec((1, total + rows, hidden), lambda i: (layer, 0, 0), pipeline_mode=pl.Buffered(1)),
        ],
        out_specs=[
            pl.BlockSpec((total, width), lambda i: (0, 0), pipeline_mode=pl.Buffered(1)),
            pl.BlockSpec((8, width), lambda i: (0, 0), pipeline_mode=pl.Buffered(1)),
        ],
        out_shape=[
            jax.ShapeDtypeStruct((total, width), jnp.bfloat16),
            jax.ShapeDtypeStruct((8, width), jnp.float32),
        ],
        scratch_shapes=[
            pltpu.VMEM((width, hidden), jnp.bfloat16),
            pltpu.VMEM((rows, hidden), jnp.float32),
            pltpu.VMEM((rows, hidden), jnp.float32),
        ],
        compiler_params=pltpu.CompilerParams(vmem_limit_bytes=VMEM_MAX),
        cost_estimate=pl.CostEstimate(
            flops=20 * 2 * total * hidden * width,
            bytes_accessed=2 * hidden * width + 7 * 4 * total * hidden,
            transcendentals=0,
        ),
        name=f"lstm_backward_{layer}",
    )(e_rows, w_stack, gates, c_all)


MESH = pl.DeviceIdType.MESH
ORDER = (7, 6, 5, 3, 4, 2, 1, 0)
AXES = ((0, 1, 2), (1, 2, 0), (2, 0, 1))


def colour_columns(width):
    tiles = width // 128
    first = -(-tiles // 3)
    second = -(-(tiles - first) // 2)
    sizes = (first * 128, second * 128, (tiles - first - second) * 128)
    return ((0, sizes[0]), (sizes[0], sizes[1]), (sizes[0] + sizes[1], sizes[2]))


def slot_one(code, axes):
    return ((code >> axes[1]) & 1) * 2 + ((code >> axes[2]) & 1)


def add_into(out_ref, a_ref, b_ref):
    @pl.loop(0, out_ref.shape[0] // 16)
    def _(i):
        at = pl.ds(pl.multiple_of(i * 16, 16), 16)
        out_ref[at, :] = a_ref[at, :] + b_ref[at, :]


def grads_kernel(
    layer, rows, hidden,
    dz_hbm, x_hbm, h_hbm, w_hbm,
    shard_ref, dx_ref,
    dz, uh, uht, w, p, r0, r1, r2, r3,
    local_sem, s0, q0, s1, q1, s2, q2, s3, q3,
):
    total, width = dz.shape
    block = 2 * hidden // 16
    me = lax.axis_index("data")
    z = lax.axis_index("replica")
    y, x, c = me // 4, lax.rem(me // 2, 2), lax.rem(me, 2)
    partner = {"replica": z, "data": y * 4 + x * 2 + 1 - c}
    across = (
        {"replica": z, "data": y * 4 + (1 - x) * 2 + c},
        {"replica": z, "data": (1 - y) * 4 + x * 2 + c},
        {"replica": 1 - z, "data": me},
    )

    u_src = x_hbm if layer == 0 else h_hbm.at[layer - 1, pl.ds(rows, total), :]
    loads = [
        pltpu.make_async_copy(u_src, uh.at[:, pl.ds(0, hidden)], local_sem.at[0]),
        pltpu.make_async_copy(h_hbm.at[layer, pl.ds(0, total), :], uh.at[:, pl.ds(hidden, hidden)], local_sem.at[1]),
        pltpu.make_async_copy(dz_hbm, dz, local_sem.at[2]),
        pltpu.make_async_copy(w_hbm.at[layer, pl.ds(0, hidden), :], w, local_sem.at[3]),
    ]
    for load in loads:
        load.start()

    barrier = pltpu.get_barrier_semaphore()
    for device in (partner,) + across:
        pl.semaphore_signal(barrier, inc=1, device_id=device, device_id_type=MESH)
    pl.semaphore_wait(barrier, 4)

    def remote(src, dst, send_sem, recv_sem, device):
        return pltpu.make_async_remote_copy(
            src_ref=src, dst_ref=dst, send_sem=send_sem, recv_sem=recv_sem, device_id=device, device_id_type=MESH
        )

    columns = colour_columns(width)
    copies = {}
    for code in range(8):
        copies[0, code] = remote(p.at[code, 1 - c], r0.at[code], s0.at[code], q0.at[code], partner)
    for k, axes in enumerate(AXES):
        cols = pl.ds(*columns[k])
        for code in range(8):
            bits = [(code >> axis) & 1 for axis in axes]
            src = p.at[code, c, :, cols]
            if bits[0]:
                slot = slot_one(code, axes)
                at = k * 4 + slot
                copies[1, k, slot] = remote(src, r1.at[slot, :, cols], s1.at[at], q1.at[at], across[axes[0]])
            elif bits[1]:
                at = k * 2 + bits[2]
                copies[2, k, bits[2]] = remote(src, r2.at[bits[2], :, cols], s2.at[at], q2.at[at], across[axes[1]])
            elif bits[2]:
                copies[3, k] = remote(src, r3.at[:, cols], s3.at[k], q3.at[k], across[axes[2]])

    loads[0].wait()
    loads[1].wait()

    @pl.loop(0, 2 * hidden // 128)
    def _(i):
        at = pl.ds(pl.multiple_of(i * 128, 128), 128)
        uht[at, :] = uh[:, at].T

    loads[2].wait()
    chunk = min(width, 1024)

    def receive_partner(code):
        copies[0, code].wait_recv()
        add_into(p.at[code, c], p.at[code, c], r0.at[code])
        for k, axes in enumerate(AXES):
            if (code >> axes[0]) & 1:
                copies[1, k, slot_one(code, axes)].start()

    before = None
    for code in ORDER:
        sides = [own + flip - 2 * own * flip for own, flip in
                 ((z, (code >> 2) & 1), (y, (code >> 1) & 1), (x, code & 1))]
        base = pl.multiple_of(((sides[0] * 2 + sides[1]) * 2 + sides[2]) * 2 * block, 2 * block)

        @pl.loop(0, width // chunk)
        def _(n):
            cols = pl.ds(pl.multiple_of(n * chunk, chunk), chunk)
            part = jnp.dot(uht[pl.ds(base, 2 * block), :], dz[:, cols], preferred_element_type=jnp.float32)
            low = part.astype(jnp.bfloat16)
            p[code, 0, :, cols] = low[:block]
            p[code, 1, :, cols] = low[block:]

        if before is not None:
            receive_partner(before)
        copies[0, code].start()
        before = code
    receive_partner(before)

    loads[3].wait()
    step = min(hidden, 512)

    @pl.loop(0, hidden // step)
    def _(n):
        at = pl.ds(pl.multiple_of(n * step, step), step)
        dx_ref[:, at] = lax.dot_general(
            dz[...], w[at, :], (((1,), (1,)), ((), ())), preferred_element_type=jnp.float32
        )

    for code in ORDER:
        for k, axes in enumerate(AXES):
            if (code >> axes[0]) & 1:
                slot = slot_one(code, axes)
                cols = pl.ds(*columns[k])
                copies[1, k, slot].wait_recv()
                here = code ^ (1 << axes[0])
                add_into(p.at[here, c, :, cols], p.at[here, c, :, cols], r1.at[slot, :, cols])
                if (here >> axes[1]) & 1:
                    copies[2, k, (here >> axes[2]) & 1].start()
    for bit in (1, 0):
        for k, axes in enumerate(AXES):
            cols = pl.ds(*columns[k])
            copies[2, k, bit].wait_recv()
            here = bit << axes[2]
            add_into(p.at[here, c, :, cols], p.at[here, c, :, cols], r2.at[bit, :, cols])
            if bit:
                copies[3, k].start()
    for k in range(3):
        cols = pl.ds(*columns[k])
        copies[3, k].wait_recv()
        add_into(shard_ref.at[:, cols], p.at[0, c, :, cols], r3.at[:, cols])
    for copy in copies.values():
        copy.wait_send()


def grads(layer, dz, x_rows, h_all, w_stack, rows):
    total, width = dz.shape
    hidden = width // 4
    block = 2 * hidden // 16
    dma = pltpu.SemaphoreType.DMA
    return pl.pallas_call(
        functools.partial(grads_kernel, layer, rows, hidden),
        in_specs=[pl.BlockSpec(memory_space=pl.ANY)] * 4,
        out_specs=[pl.BlockSpec(memory_space=pltpu.VMEM)] * 2,
        out_shape=[
            jax.ShapeDtypeStruct((block, width), jnp.bfloat16),
            jax.ShapeDtypeStruct((total, hidden), jnp.float32),
        ],
        scratch_shapes=[
            pltpu.VMEM((total, width), jnp.bfloat16),
            pltpu.VMEM((total, 2 * hidden), jnp.bfloat16),
            pltpu.VMEM((2 * hidden, total), jnp.bfloat16),
            pltpu.VMEM((hidden, width), jnp.bfloat16),
            pltpu.VMEM((8, 2, block, width), jnp.bfloat16),
            pltpu.VMEM((8, block, width), jnp.bfloat16),
            pltpu.VMEM((4, block, width), jnp.bfloat16),
            pltpu.VMEM((2, block, width), jnp.bfloat16),
            pltpu.VMEM((block, width), jnp.bfloat16),
            dma((4,)), dma((8,)), dma((8,)), dma((12,)), dma((12,)), dma((6,)), dma((6,)), dma((3,)), dma((3,)),
        ],
        compiler_params=pltpu.CompilerParams(
            collective_id=layer, has_side_effects=True, vmem_limit_bytes=VMEM_MAX
        ),
        cost_estimate=pl.CostEstimate(
            flops=6 * total * hidden * width * 5, bytes_accessed=8 * hidden * width, transcendentals=0
        ),
        name=f"lstm_grads_{layer}",
    )(dz, x_rows, h_all, w_stack)


def widen_kernel(part_ref, *refs):
    refs[-1][0] = part_ref[...].astype(jnp.float32)


def widen(total, part, layer, layers):
    height, width = part.shape
    block = min(height, 256)
    return pl.pallas_call(
        widen_kernel,
        grid=(height // block,),
        in_specs=[pl.BlockSpec((block, width), lambda i: (i, 0))]
        + ([] if total is None else [pl.BlockSpec(memory_space=pl.ANY)]),
        out_specs=pl.BlockSpec((1, block, width), lambda i: (layer, i, 0)),
        out_shape=jax.ShapeDtypeStruct((layers, height, width), jnp.float32),
        input_output_aliases={} if total is None else {1: 0},
        cost_estimate=pl.CostEstimate(flops=height * width, bytes_accessed=6 * height * width, transcendentals=0),
        name=f"widen_{layer}",
    )(*([part] if total is None else [part, total]))


def solution(mesh):
    batch_axes = ("replica", "data")

    def local_grads(x_loc, dy_loc, w_stack, b_stack):
        layers, _, width = w_stack.shape
        hidden = width // 4
        rows, steps, _ = x_loc.shape
        x_rows = jnp.swapaxes(x_loc, 0, 1).reshape(steps * rows, hidden)
        e_rows = jnp.swapaxes(dy_loc, 0, 1).reshape(steps * rows, hidden)
        h_all, gates, c_all = forward(x_rows, w_stack, b_stack, rows)
        db_list = []
        dw_sum = None
        waiting = None
        for layer in reversed(range(layers)):
            dz, db = backward(layer, e_rows, w_stack, gates, c_all, rows)
            db_list.append(jnp.sum(db, axis=0))
            shard, e_rows = grads(layer, dz, x_rows, h_all, w_stack, rows)
            if waiting is not None:
                summed, shard = lax.optimization_barrier((waiting, shard))
                dw_sum = widen(dw_sum, summed, layer + 1, layers)
            waiting = lax.all_gather(shard, batch_axes, axis=0, tiled=True)
        db_sum = lax.psum(jnp.stack(db_list[::-1]).astype(jnp.bfloat16), batch_axes).astype(jnp.float32)
        dw_sum = widen(dw_sum, waiting, 0, layers)
        dx = jnp.swapaxes(e_rows.reshape(steps, rows, hidden), 0, 1)
        return dw_sum, db_sum, dx

    return jax.shard_map(
        local_grads,
        mesh=mesh,
        in_specs=(P(batch_axes), P(batch_axes), P(), P()),
        out_specs=(P(), P(), P(batch_axes)),
        check_vma=False,
    )
```

time: 2020 us -> 768 us (0.38)
  matrix products: 835 us -> 0 us
  Pallas kernels: 0 us -> 704 us
  waiting for transfers between devices: 616 us -> 0.13 us
  other arithmetic: 395 us -> 2.75 us
  local copies, waits for them, and re-layouts: 106 us -> 12.6 us
    dot_general x144 -> x0, matrix products: 835 us -> none  [the longest x64 381 us: time_step(): jnp.einsum('bg,hg->bh', dz_low, w_rec, preferred_element_type=jnp.float32)]
    pallas_call x0 -> x13, Pallas kernels: none -> 704 us  [the longest x4 347 us: grads(): pl.pallas_call(functools.partial(grads_kernel, layer, rows, hidden), in_s...]
    all_gather x4, waiting for transfers between devices: 305 us -> 0.06 us  [local_grads(): waiting = lax.all_gather(shard, batch_axes, axis=0, tiled=True)]
    psum x1 -> x0, waiting for transfers between devices: 197 us -> none  [reduce_weights(): shard_sum = lax.psum(shard_sum, 'replica')]
    concatenate x132 -> x0, other arithmetic: 178 us -> none  [the longest x128 150 us: time_step(): jnp.concatenate([dc_cur * gate_g * gate_i * (1.0 - gate_i), dc_cur * c_pr...]
    dynamic_update_slice x192 -> x0, other arithmetic: 149 us -> none  [the longest x128 103 us: layer_forward(): return lax.scan(time_step, init_state, in_proj)[1]]
    reduce_scatter x4 -> x0, waiting for transfers between devices: 113 us -> none  [reduce_weights(): lax.psum_scatter(part_low, 'data', scatter_dimension=0, tiled=True)]
    another operation x2 -> x1, other arithmetic: 64.2 us -> 0.09 us  [local_grads(): jnp.stack(db_list[::-1]).astype(jnp.bfloat16)]
  transfers between devices with their start and end apart: 9 -> 4, of which waited for: 6 -> 0; matrix products, arithmetic and copies ran while one was open for 28% -> 1% of each run, Pallas kernels for 0% -> 58%
where the time goes in v1:
time: 768 us; the launch traced here: 767 us
  Pallas kernels  704 us (92%)
  blocking collectives  32.7 us (4%)
  between operations  13.9 us (2%)
  local copies, waits for them, and re-layouts  12.6 us (2%)
    pallas_call x4, Pallas kernels, grads(): pl.pallas_call(functools.partial(grads_kernel, layer, rows, hidden), in_s...  347 us
    pallas_call x4, Pallas kernels, backward(): pl.pallas_call(functools.partial(backward_kernel, rows, steps, hidden), g...  144 us
    pallas_call x1, Pallas kernels, forward(): pl.pallas_call(functools.partial(forward_kernel, rows, steps, hidden), gr...  140 us
    pallas_call x4, Pallas kernels, widen(): pl.pallas_call(widen_kernel, grid=(height // block,), in_specs=[pl.BlockS...  73.1 us
    psum x1, blocking collectives, local_grads(): lax.psum(jnp.stack(db_list[::-1]).astype(jnp.bfloat16), batch_axes)  32.7 us
  transfers between devices with their start and end apart: 4, of which 0 were waited for; matrix products, arithmetic and copies ran while one was open for 1% of the time, Pallas kernels for 58%

profile of v1, /device:TPU:0, one launch (start us, length us, event | category | flops | bytes accessed | tf_op | source)
XLA Modules:
  0.0 767.0 jit_solution(10522974750675335688)
XLA Ops:
  7.2 0.0 all-gather.5.cloned.1.call-start
  7.2 1.5 reshape.20.b_ref
  8.7 2.8 copy.11
  11.5 4.1 copy.10
  15.6 140.3 %lstm_forward.1 = (bf16[4,544,1024]{2,1,0:T(8,128)(2,1)}, f32[4,512,4096]{2,1,0:T(8,128)}, f32[4,544,1024]{2,1,0:T(8,128)}) custom-call(bf16[512,1024]{1,0:T(8,128)(2,1)} %bitcast.13, bf16[4,2048,4096]{2,1,0:T(8,128)(2,1)} %w_hbm.7, f32[4,1,4096]{2,1,0:T(1,128)} %reshape.20.b_ref), custom_call_target="tpu_custom_call" | custom-call | flops 34359738368 | bytes 75497472 | tf_op jit(solution)/shard_map/lstm_forward/pallas_call | solution.py:59
  156.0 36.0 %lstm_backward_3.1 = (bf16[512,4096]{1,0:T(8,128)(2,1)}, f32[8,4096]{1,0:T(8,128)}) custom-call(f32[512,1024]{1,0:T(8,128)} %bitcast.11, bf16[4,2048,4096]{2,1,0:T(8,128)(2,1)} %w_hbm.7, f32[4,512,4096]{2,1,0:T(8,128)} %get-tuple-element.28.gates_ref, f32[4,544,1024]{2,1,0:T(8,128)} %get-tuple-element.29.c_ref), custom_call_target="tpu_custom_call" | custom-call | flops 85899345920 | bytes 23068672 | tf_op jit(solution)/shard_map/lstm_backward_3/pallas_call | solution.py:141
  192.0 67.3 %lstm_grads_3.1 = (bf16[128,4096]{1,0:T(8,128)(2,1)}, f32[512,1024]{1,0:T(8,128)}) custom-call(bf16[512,4096]{1,0:T(8,128)(2,1)} %get-tuple-element.30.dz_hbm, bf16[512,1024]{1,0:T(8,128)(2,1)} %bitcast.14, bf16[4,544,1024]{2,1,0:T(8,128)(2,1)} %get-tuple-element.31.h_hbm, bf16[4,2048,4096]{2,1,0:T(8,128)(2,1)} %w_hbm.7), custom_call_target="tpu_custom_call" | custom-call | flops 64424509440 | bytes 33554432 | tf_op jit(solution)/shard_map/lstm_grads_3/pallas_call | solution.py:334
  259.3 0.0 all-gather.5.cloned.1.call-update
  259.3 0.2 all-gather.7.cloned.1.call-start
  259.5 36.1 %lstm_backward_2.1 = (bf16[512,4096]{1,0:T(8,128)(2,1)}, f32[8,4096]{1,0:T(8,128)}) custom-call(f32[512,1024]{1,0:T(8,128)} %get-tuple-element.33.e_ref, bf16[4,2048,4096]{2,1,0:T(8,128)(2,1)} %w_hbm.7, f32[4,512,4096]{2,1,0:T(8,128)} %get-tuple-element.28.gates_ref, f32[4,544,1024]{2,1,0:T(8,128)} %get-tuple-element.29.c_ref), custom_call_target="tpu_custom_call" | custom-call | flops 85899345920 | bytes 23068672 | tf_op jit(solution)/shard_map/lstm_backward_2/pallas_call | solution.py:141
  295.6 93.1 %lstm_grads_2.1 = (bf16[128,4096]{1,0:T(8,128)(2,1)}, f32[512,1024]{1,0:T(8,128)}) custom-call(bf16[512,4096]{1,0:T(8,128)(2,1)} %get-tuple-element.34.dz_hbm, bf16[512,1024]{1,0:T(8,128)(2,1)} %bitcast.15, bf16[4,544,1024]{2,1,0:T(8,128)(2,1)} %get-tuple-element.31.h_hbm, bf16[4,2048,4096]{2,1,0:T(8,128)(2,1)} %w_hbm.7), custom_call_target="tpu_custom_call" | custom-call | flops 64424509440 | bytes 33554432 | tf_op jit(solution)/shard_map/lstm_grads_2/pallas_call | solution.py:334
  388.7 0.0 all-gather.5.cloned.1.call-done.part_ref
  388.8 0.0 all-gather.7.cloned.1.call-update
  388.8 0.0 all-gather.9.cloned.1.call-start
  388.8 36.1 %lstm_backward_1.1 = (bf16[512,4096]{1,0:T(8,128)(2,1)}, f32[8,4096]{1,0:T(8,128)}) custom-call(f32[512,1024]{1,0:T(8,128)} %get-tuple-element.37.e_ref, bf16[4,2048,4096]{2,1,0:T(8,128)(2,1)} %w_hbm.7, f32[4,512,4096]{2,1,0:T(8,128)} %get-tuple-element.28.gates_ref, f32[4,544,1024]{2,1,0:T(8,128)} %get-tuple-element.29.c_ref), custom_call_target="tpu_custom_call" | custom-call | flops 85899345920 | bytes 23068672 | tf_op jit(solution)/shard_map/lstm_backward_1/pallas_call | solution.py:141
  425.0 93.2 %lstm_grads_1.1 = (bf16[128,4096]{1,0:T(8,128)(2,1)}, f32[512,1024]{1,0:T(8,128)}) custom-call(bf16[512,4096]{1,0:T(8,128)(2,1)} %get-tuple-element.38.dz_hbm, bf16[512,1024]{1,0:T(8,128)(2,1)} %bitcast.16, bf16[4,544,1024]{2,1,0:T(8,128)(2,1)} %get-tuple-element.31.h_hbm, bf16[4,2048,4096]{2,1,0:T(8,128)(2,1)} %w_hbm.7), custom_call_target="tpu_custom_call" | custom-call | flops 64424509440 | bytes 33554432 | tf_op jit(solution)/shard_map/lstm_grads_1/pallas_call | solution.py:334
  518.2 0.0 all-gather.7.cloned.1.call-done.part_ref
  518.2 0.0 all-gather.9.cloned.1.call-update
  518.3 0.3 all-gather.11.cloned.1.call-start
  518.5 36.1 %lstm_backward_0.1 = (bf16[512,4096]{1,0:T(8,128)(2,1)}, f32[8,4096]{1,0:T(8,128)}) custom-call(f32[512,1024]{1,0:T(8,128)} %get-tuple-element.41.e_ref, bf16[4,2048,4096]{2,1,0:T(8,128)(2,1)} %w_hbm.7, f32[4,512,4096]{2,1,0:T(8,128)} %get-tuple-element.28.gates_ref, f32[4,544,1024]{2,1,0:T(8,128)} %get-tuple-element.29.c_ref), custom_call_target="tpu_custom_call" | custom-call | flops 85899345920 | bytes 23068672 | tf_op jit(solution)/shard_map/lstm_backward_0/pallas_call | solution.py:141
  554.6 93.0 %lstm_grads_0.1 = (bf16[128,4096]{1,0:T(8,128)(2,1)}, f32[512,1024]{1,0:T(8,128)}) custom-call(bf16[512,4096]{1,0:T(8,128)(2,1)} %get-tuple-element.42.dz_hbm, bf16[512,1024]{1,0:T(8,128)(2,1)} %bitcast.17, bf16[4,544,1024]{2,1,0:T(8,128)(2,1)} %get-tuple-element.31.h_hbm, bf16[4,2048,4096]{2,1,0:T(8,128)(2,1)} %w_hbm.7), custom_call_target="tpu_custom_call" | custom-call | flops 64424509440 | bytes 33554432 | tf_op jit(solution)/shard_map/lstm_grads_0/pallas_call | solution.py:334
  647.6 0.0 copy-start.1
  647.6 0.0 copy-start
  647.6 0.0 all-gather.9.cloned.1.call-done.part_ref
  647.6 0.0 all-gather.11.cloned.1.call-update
  647.7 1.0 reduce_sum.39
  648.7 0.9 reduce_sum.38
  649.6 4.1 copy.14
  653.8 0.0 copy-done.1
  653.8 0.0 copy-done
  653.9 0.1 pad_maximum_fusion
  654.0 32.7 %psum.7 = bf16[4,4096]{1,0:T(4,128)(2,1)S(1)} all-reduce(bf16[4,4096]{1,0:T(4,128)(2,1)S(1)} %pad_maximum_fusion), channel_id=1, replica_groups=mesh['replica'=2,'data'=8] {'replica','data'}, use_global_device_ids=true, to_apply=%region_4.0 | all-reduce | flops 16384 | bytes 65536 | tf_op jit(solution)/shard_map/psum | solution.py:405
  686.7 0.6 convert_element_type.4
  687.3 18.3 %widen_3.1.refs_0_ = f32[4,2048,4096]{2,1,0:T(8,128)} custom-call(bf16[2048,4096]{1,0:T(8,128)(2,1)} %all-gather.5.cloned.1.call-done.part_ref), custom_call_target="tpu_custom_call" | custom-call | flops 8388608 | bytes 50331648 | tf_op jit(solution)/shard_map/widen_3/pallas_call | solution.py:371
  705.6 18.3 %widen_2.1.refs_0_ = f32[4,2048,4096]{2,1,0:T(8,128)} custom-call(bf16[2048,4096]{1,0:T(8,128)(2,1)} %all-gather.7.cloned.1.call-done.part_ref, f32[4,2048,4096]{2,1,0:T(8,128)} %widen_3.1.refs_0_), custom_call_target="tpu_custom_call", output_to_operand_aliasing={{}: (1, {})} | custom-call | flops 8388608 | bytes 50331648 | tf_op jit(solution)/shard_map/widen_2/pallas_call | solution.py:371
  723.9 18.3 %widen_1.1.refs_0_ = f32[4,2048,4096]{2,1,0:T(8,128)} custom-call(bf16[2048,4096]{1,0:T(8,128)(2,1)} %all-gather.9.cloned.1.call-done.part_ref, f32[4,2048,4096]{2,1,0:T(8,128)} %widen_2.1.refs_0_), custom_call_target="tpu_custom_call", output_to_operand_aliasing={{}: (1, {})} | custom-call | flops 8388608 | bytes 50331648 | tf_op jit(solution)/shard_map/widen_1/pallas_call | solution.py:371
  742.2 0.0 all-gather.11.cloned.1.call-done.part_ref
  742.2 18.3 %widen_0.1 = f32[4,2048,4096]{2,1,0:T(8,128)} custom-call(bf16[2048,4096]{1,0:T(8,128)(2,1)} %all-gather.11.cloned.1.call-done.part_ref, f32[4,2048,4096]{2,1,0:T(8,128)} %widen_1.1.refs_0_), custom_call_target="tpu_custom_call", output_to_operand_aliasing={{}: (1, {})} | custom-call | flops 8388608 | bytes 50331648 | tf_op jit(solution)/shard_map/widen_0/pallas_call | solution.py:371
  (6 shorter events, 0.1 us)
Async XLA Ops:
  7.2 381.6 %all-gather.5.cloned.1.call-start = ((), (), s32[]{:S(2)}) async-start(), calls=%async_computation | async-start | bytes 17825792 | tf_op jit(solution)/shard_map/all_gather | solution.py:404
  259.3 258.9 %all-gather.7.cloned.1.call-start = ((), (), s32[]{:S(2)}) async-start(), calls=%async_computation.1 | async-start | bytes 17825792 | tf_op jit(solution)/shard_map/all_gather | solution.py:404
  388.8 258.8 %all-gather.9.cloned.1.call-start = ((), (), s32[]{:S(2)}) async-start(), calls=%async_computation.2 | async-start | bytes 17825792 | tf_op jit(solution)/shard_map/all_gather | solution.py:404
  518.3 223.9 %all-gather.11.cloned.1.call-start = ((), (), s32[]{:S(2)}) async-start(), calls=%async_computation.3 | async-start | bytes 17825792 | tf_op jit(solution)/shard_map/all_gather | solution.py:404
  647.6 6.2 copy-start.1
  647.6 6.2 copy-start
Sparse Core Ops, SparseCore 0:
  259.4 103.2 all-gather.4
  388.9 103.2 all-gather.6
  518.4 102.8 all-gather.8
  647.8 77.4 all-gather.10

commit v2 on v1

--- a/solution.py
+++ b/solution.py
@@ -27,7 +27,7 @@
     def _(n):
         cols = pl.ds(pl.multiple_of(n * BLK, BLK), BLK)
         part = jnp.dot(u_ref[...], w_ref[0, :hidden, cols], preferred_element_type=jnp.float32)
-        gates_ref[0, :, cols] = part + b_ref[0, :, cols]
+        gates_ref[0, :, cols] = part + b_ref[pl.ds(pl.program_id(0), 1), cols]
 
     @pl.loop(0, steps)
     def _(t):
@@ -62,7 +62,7 @@
         in_specs=[
             pl.BlockSpec((total, hidden), lambda l: (0, 0)),
             pl.BlockSpec((1, 2 * hidden, width), lambda l: (l, 0, 0)),
-            pl.BlockSpec((1, 1, width), lambda l: (l, 0, 0)),
+            pl.BlockSpec((layers, width), lambda l: (0, 0)),
         ],
         out_specs=[
             pl.BlockSpec((1, total + rows, hidden), lambda l: (l, 0, 0)),
@@ -82,19 +82,52 @@
             transcendentals=0,
         ),
         name="lstm_forward",
-    )(x_rows, w_stack, b_stack.reshape(layers, 1, width))
-
-
-def backward_kernel(rows, steps, hidden, e_ref, w_ref, gates_ref, c_ref, dz_ref, db_ref, wt_ref, r_ref, dc_ref):
-    blocks = hidden // BLK
-
-    @pl.loop(0, blocks)
+    )(x_rows, w_stack, b_stack)
+
+
+def backward_step(rows, hidden, t, gate, e_ref, c, wt_ref, r_ref, dc_ref, dz_ref, db_ref):
+    now = pl.ds(pl.multiple_of(t * rows, rows), rows)
+    later = pl.ds(pl.multiple_of(t * rows + rows, rows), rows)
+    total = None
+    for j in range(hidden // BLK):
+        part = pl.ds(j * BLK, BLK)
+        cols = [pl.ds(k * hidden + j * BLK, BLK) for k in range(4)]
+        gate_i, gate_f, gate_g, gate_o = [gate(col) for col in cols]
+        tanh_c = jnp.tanh(c(later, part))
+        dh = e_ref[now, part] + r_ref[:, part]
+        dc = dc_ref[:, part] + dh * gate_o * (1.0 - tanh_c * tanh_c)
+        dz = [
+            dc * gate_g * gate_i * (1.0 - gate_i),
+            dc * c(now, part) * gate_f * (1.0 - gate_f),
+            dc * gate_i * (1.0 - gate_g * gate_g),
+            dh * tanh_c * gate_o * (1.0 - gate_o),
+        ]
+        dc_ref[:, part] = dc * gate_f
+        low = []
+        for col, value in zip(cols, dz):
+            low.append(value.astype(jnp.bfloat16))
+            dz_ref[now, col] = low[-1]
+            db_ref[:, col] += jnp.sum(value.reshape(rows // 8, 8, BLK), axis=0)
+        back = jnp.dot(
+            jnp.concatenate(low, axis=1),
+            wt_ref[j * 4 * BLK : (j + 1) * 4 * BLK, :],
+            preferred_element_type=jnp.float32,
+        )
+        total = back if total is None else total + back
+    r_ref[...] = total
+
+
+def transpose_recurrent(hidden, w, wt_ref):
+    @pl.loop(0, hidden // BLK)
     def _(j):
         for k in range(4):
             cols = pl.ds(pl.multiple_of(k * hidden + j * BLK, BLK), BLK)
             place = pl.ds(pl.multiple_of(j * 4 * BLK + k * BLK, BLK), BLK)
-            wt_ref[place, :] = w_ref[0, :, cols].T
-
+            wt_ref[place, :] = w(cols).T
+
+
+def backward_kernel(rows, steps, hidden, e_ref, w_ref, gates_ref, c_ref, dz_ref, db_ref, wt_ref, r_ref, dc_ref):
+    transpose_recurrent(hidden, lambda cols: w_ref[0, :, cols], wt_ref)
     r_ref[...] = jnp.zeros_like(r_ref)
     dc_ref[...] = jnp.zeros_like(dc_ref)
     db_ref[...] = jnp.zeros_like(db_ref)
@@ -103,34 +136,10 @@
     def _(s):
         t = steps - 1 - s
         now = pl.ds(pl.multiple_of(t * rows, rows), rows)
-        later = pl.ds(pl.multiple_of(t * rows + rows, rows), rows)
-        total = None
-        for j in range(blocks):
-            part = pl.ds(j * BLK, BLK)
-            cols = [pl.ds(k * hidden + j * BLK, BLK) for k in range(4)]
-            gate_i, gate_f, gate_g, gate_o = [gates_ref[0, now, col] for col in cols]
-            tanh_c = jnp.tanh(c_ref[0, later, part])
-            dh = e_ref[now, part] + r_ref[:, part]
-            dc = dc_ref[:, part] + dh * gate_o * (1.0 - tanh_c * tanh_c)
-            dz = [
-                dc * gate_g * gate_i * (1.0 - gate_i),
-                dc * c_ref[0, now, part] * gate_f * (1.0 - gate_f),
-                dc * gate_i * (1.0 - gate_g * gate_g),
-                dh * tanh_c * gate_o * (1.0 - gate_o),
-            ]
-            dc_ref[:, part] = dc * gate_f
-            low = []
-            for col, value in zip(cols, dz):
-                low.append(value.astype(jnp.bfloat16))
-                dz_ref[now, col] = low[-1]
-                db_ref[:, col] += jnp.sum(value.reshape(rows // 8, 8, BLK), axis=0)
-            back = jnp.dot(
-                jnp.concatenate(low, axis=1),
-                wt_ref[j * 4 * BLK : (j + 1) * 4 * BLK, :],
-                preferred_element_type=jnp.float32,
-            )
-            total = back if total is None else total + back
-        r_ref[...] = total
+        backward_step(
+            rows, hidden, t, lambda col: gates_ref[0, now, col], e_ref, lambda at, col: c_ref[0, at, col],
+            wt_ref, r_ref, dc_ref, dz_ref, db_ref,
+        )
 
 
 def backward(layer, e_rows, w_stack, gates, c_all, rows):
@@ -194,15 +203,21 @@
         out_ref[at, :] = a_ref[at, :] + b_ref[at, :]
 
 
-def grads_kernel(
-    layer, rows, hidden,
-    dz_hbm, x_hbm, h_hbm, w_hbm,
-    shard_ref, dx_ref,
-    dz, uh, uht, w, p, r0, r1, r2, r3,
-    local_sem, s0, q0, s1, q1, s2, q2, s3, q3,
-):
+def grads_kernel(layer, rows, hidden, dz_hbm, db_hbm, x_hbm, h_hbm, w_hbm, gates_hbm, c_hbm, *refs):
+    below = layer - 1
+    if layer:
+        shard_ref, dbsum_ref, dz_out, db_ref, *refs = refs
+        dz, uh, uht, w, p, r0, r1, r2, r3, db8, part_db, got_db, *refs = refs
+        local_sem, s0, q0, s1, q1, s2, q2, s3, q3, sd, qd, *refs = refs
+        dx_ref, c_all, ring, r_ref, dc_ref, ring_sem = refs
+    else:
+        shard_ref, dbsum_ref, dx_ref, *refs = refs
+        dz, uh, uht, w, p, r0, r1, r2, r3, db8, part_db, got_db, *refs = refs
+        local_sem, s0, q0, s1, q1, s2, q2, s3, q3, sd, qd = refs
     total, width = dz.shape
+    steps = total // rows
     block = 2 * hidden // 16
+    parts = width // hidden
     me = lax.axis_index("data")
     z = lax.axis_index("replica")
     y, x, c = me // 4, lax.rem(me // 2, 2), lax.rem(me, 2)
@@ -213,15 +228,27 @@
         {"replica": 1 - z, "data": me},
     )
 
-    u_src = x_hbm if layer == 0 else h_hbm.at[layer - 1, pl.ds(rows, total), :]
+    u_src = x_hbm if layer == 0 else h_hbm.at[below, pl.ds(rows, total), :]
     loads = [
         pltpu.make_async_copy(u_src, uh.at[:, pl.ds(0, hidden)], local_sem.at[0]),
         pltpu.make_async_copy(h_hbm.at[layer, pl.ds(0, total), :], uh.at[:, pl.ds(hidden, hidden)], local_sem.at[1]),
         pltpu.make_async_copy(dz_hbm, dz, local_sem.at[2]),
-        pltpu.make_async_copy(w_hbm.at[layer, pl.ds(0, hidden), :], w, local_sem.at[3]),
+        pltpu.make_async_copy(db_hbm, db8, local_sem.at[3]),
+        pltpu.make_async_copy(w_hbm.at[layer, pl.ds(0, hidden), :], w, local_sem.at[4]),
     ]
+    if layer:
+        loads.append(pltpu.make_async_copy(c_hbm.at[below], c_all, local_sem.at[5]))
     for load in loads:
         load.start()
+
+    def gates_load(s, slot):
+        at = pl.ds(pl.multiple_of((steps - 1 - s) * rows, rows), rows)
+        return pltpu.make_async_copy(gates_hbm.at[below, at, :], ring.at[slot], ring_sem.at[slot])
+
+    depth = 4
+    if layer:
+        for s in range(min(depth, steps)):
+            gates_load(s, s).start()
 
     barrier = pltpu.get_barrier_semaphore()
     for device in (partner,) + across:
@@ -236,7 +263,10 @@
     columns = colour_columns(width)
     copies = {}
     for code in range(8):
-        copies[0, code] = remote(p.at[code, 1 - c], r0.at[code], s0.at[code], q0.at[code], partner)
+        for n in range(parts):
+            at = code * parts + n
+            src = p.at[code, 1 - c, :, pl.ds(n * hidden, hidden)]
+            copies[0, code, n] = remote(src, r0.at[pl.ds(at * block, block), :], s0.at[at], q0.at[at], partner)
     for k, axes in enumerate(AXES):
         cols = pl.ds(*columns[k])
         for code in range(8):
@@ -251,7 +281,18 @@
                 copies[2, k, bits[2]] = remote(src, r2.at[bits[2], :, cols], s2.at[at], q2.at[at], across[axes[1]])
             elif bits[2]:
                 copies[3, k] = remote(src, r3.at[:, cols], s3.at[k], q3.at[k], across[axes[2]])
-
+    for stage, device in enumerate((partner,) + across):
+        copies[4, stage] = remote(part_db.at[stage], got_db.at[stage], sd.at[stage], qd.at[stage], device)
+
+    def bias_stage(stage):
+        copies[4, stage].wait_recv()
+        out = part_db.at[stage + 1] if stage < 3 else dbsum_ref
+        out[...] = part_db[stage] + got_db[stage]
+        if stage < 3:
+            copies[4, stage + 1].start()
+
+    loads[3].wait()
+    part_db[0] = jnp.sum(db8[...], axis=0, keepdims=True).astype(jnp.bfloat16).astype(jnp.float32)
     loads[0].wait()
     loads[1].wait()
 
@@ -260,20 +301,26 @@
         at = pl.ds(pl.multiple_of(i * 128, 128), 128)
         uht[at, :] = uh[:, at].T
 
+    copies[4, 0].start()
     loads[2].wait()
     chunk = min(width, 1024)
 
     def receive_partner(code):
-        copies[0, code].wait_recv()
-        add_into(p.at[code, c], p.at[code, c], r0.at[code])
+        for n in range(parts):
+            copies[0, code, n].wait_recv()
+            cols = pl.ds(n * hidden, hidden)
+            mine = p.at[code, c, :, cols]
+            add_into(mine, mine, r0.at[pl.ds((code * parts + n) * block, block), :])
         for k, axes in enumerate(AXES):
             if (code >> axes[0]) & 1:
                 copies[1, k, slot_one(code, axes)].start()
 
     before = None
     for code in ORDER:
-        sides = [own + flip - 2 * own * flip for own, flip in
-                 ((z, (code >> 2) & 1), (y, (code >> 1) & 1), (x, code & 1))]
+        sides = [
+            own + flip - 2 * own * flip
+            for own, flip in ((z, (code >> 2) & 1), (y, (code >> 1) & 1), (x, code & 1))
+        ]
         base = pl.multiple_of(((sides[0] * 2 + sides[1]) * 2 + sides[2]) * 2 * block, 2 * block)
 
         @pl.loop(0, width // chunk)
@@ -286,11 +333,13 @@
 
         if before is not None:
             receive_partner(before)
-        copies[0, code].start()
+        for n in range(parts):
+            copies[0, code, n].start()
         before = code
     receive_partner(before)
-
-    loads[3].wait()
+    bias_stage(0)
+
+    loads[4].wait()
     step = min(hidden, 512)
 
     @pl.loop(0, hidden // step)
@@ -300,57 +349,127 @@
             dz[...], w[at, :], (((1,), (1,)), ((), ())), preferred_element_type=jnp.float32
         )
 
-    for code in ORDER:
-        for k, axes in enumerate(AXES):
-            if (code >> axes[0]) & 1:
-                slot = slot_one(code, axes)
-                cols = pl.ds(*columns[k])
-                copies[1, k, slot].wait_recv()
-                here = code ^ (1 << axes[0])
-                add_into(p.at[here, c, :, cols], p.at[here, c, :, cols], r1.at[slot, :, cols])
-                if (here >> axes[1]) & 1:
-                    copies[2, k, (here >> axes[2]) & 1].start()
+    def first_crossing(codes):
+        for code in codes:
+            for k, axes in enumerate(AXES):
+                if (code >> axes[0]) & 1:
+                    slot = slot_one(code, axes)
+                    cols = pl.ds(*columns[k])
+                    copies[1, k, slot].wait_recv()
+                    here = code ^ (1 << axes[0])
+                    mine = p.at[here, c, :, cols]
+                    add_into(mine, mine, r1.at[slot, :, cols])
+                    if (here >> axes[1]) & 1:
+                        copies[2, k, (here >> axes[2]) & 1].start()
+
+    bias_stage(1)
+    if layer:
+        reload = pltpu.make_async_copy(w_hbm.at[below, pl.ds(hidden, hidden), :], w, local_sem.at[4])
+        reload.start()
+        r_ref[...] = jnp.zeros_like(r_ref)
+        dc_ref[...] = jnp.zeros_like(dc_ref)
+        db_ref[...] = jnp.zeros_like(db_ref)
+        loads[5].wait()
+        reload.wait()
+        transpose_recurrent(hidden, lambda cols: w[:, cols], r0)
+
+        @pl.loop(0, steps)
+        def _(s):
+            slot = lax.rem(s, depth)
+            gates_load(s, slot).wait()
+            backward_step(
+                rows, hidden, steps - 1 - s, lambda col: ring[slot, :, col], dx_ref,
+                lambda at, col: c_all[at, col], r0, r_ref, dc_ref, dz, db_ref,
+            )
+
+            @pl.when(s + depth < steps)
+            def _():
+                gates_load(s + depth, slot).start()
+
+            @pl.when(s == steps // 2 - 2)
+            def _():
+                first_crossing(ORDER[:1])
+
+            @pl.when(s == steps - 3)
+            def _():
+                first_crossing(ORDER[1:4])
+
+        store = pltpu.make_async_copy(dz, dz_out, local_sem.at[2])
+        store.start()
+        first_crossing(ORDER[4:])
+    else:
+        first_crossing(ORDER)
+    bias_stage(2)
     for bit in (1, 0):
         for k, axes in enumerate(AXES):
             cols = pl.ds(*columns[k])
             copies[2, k, bit].wait_recv()
-            here = bit << axes[2]
-            add_into(p.at[here, c, :, cols], p.at[here, c, :, cols], r2.at[bit, :, cols])
+            mine = p.at[bit << axes[2], c, :, cols]
+            add_into(mine, mine, r2.at[bit, :, cols])
             if bit:
                 copies[3, k].start()
+    bias_stage(3)
     for k in range(3):
         cols = pl.ds(*columns[k])
         copies[3, k].wait_recv()
         add_into(shard_ref.at[:, cols], p.at[0, c, :, cols], r3.at[:, cols])
     for copy in copies.values():
         copy.wait_send()
-
-
-def grads(layer, dz, x_rows, h_all, w_stack, rows):
+    if layer:
+        store.wait()
+
+
+def grads(layer, dz, db, x_rows, h_all, w_stack, gates, c_all, rows):
     total, width = dz.shape
     hidden = width // 4
     block = 2 * hidden // 16
+    parts = 8 * (width // hidden)
     dma = pltpu.SemaphoreType.DMA
+    vmem = pl.BlockSpec(memory_space=pltpu.VMEM)
+    hbm = pl.BlockSpec(memory_space=pl.ANY)
+    out_shape = [
+        jax.ShapeDtypeStruct((block, width), jnp.bfloat16),
+        jax.ShapeDtypeStruct((1, width), jnp.float32),
+    ]
+    scratch = [
+        pltpu.VMEM((total, width), jnp.bfloat16),
+        pltpu.VMEM((total, 2 * hidden), jnp.bfloat16),
+        pltpu.VMEM((2 * hidden, total), jnp.bfloat16),
+        pltpu.VMEM((hidden, width), jnp.bfloat16),
+        pltpu.VMEM((8, 2, block, width), jnp.bfloat16),
+        pltpu.VMEM((width, hidden), jnp.bfloat16),
+        pltpu.VMEM((4, block, width), jnp.bfloat16),
+        pltpu.VMEM((2, block, width), jnp.bfloat16),
+        pltpu.VMEM((block, width), jnp.bfloat16),
+        pltpu.VMEM((8, width), jnp.float32),
+        pltpu.VMEM((4, 1, width), jnp.float32),
+        pltpu.VMEM((4, 1, width), jnp.float32),
+        dma((6,)), dma((parts,)), dma((parts,)), dma((12,)), dma((12,)), dma((6,)), dma((6,)), dma((3,)), dma((3,)),
+        dma((4,)), dma((4,)),
+    ]
+    if layer:
+        out_specs = [vmem, vmem, hbm, vmem]
+        out_shape += [
+            jax.ShapeDtypeStruct((total, width), jnp.bfloat16),
+            jax.ShapeDtypeStruct((8, width), jnp.float32),
+        ]
+        scratch += [
+            pltpu.VMEM((total, hidden), jnp.float32),
+            pltpu.VMEM((total + rows, hidden), jnp.float32),
+            pltpu.VMEM((4, rows, width), jnp.float32),
+            pltpu.VMEM((rows, hidden), jnp.float32),
+            pltpu.VMEM((rows, hidden), jnp.float32),
+            dma((4,)),
+        ]
+    else:
+        out_specs = [vmem, vmem, vmem]
+        out_shape += [jax.ShapeDtypeStruct((total, hidden), jnp.float32)]
     return pl.pallas_call(
         functools.partial(grads_kernel, layer, rows, hidden),
-        in_specs=[pl.BlockSpec(memory_space=pl.ANY)] * 4,
-        out_specs=[pl.BlockSpec(memory_space=pltpu.VMEM)] * 2,
-        out_shape=[
-            jax.ShapeDtypeStruct((block, width), jnp.bfloat16),
-            jax.ShapeDtypeStruct((total, hidden), jnp.float32),
-        ],
-        scratch_shapes=[
-            pltpu.VMEM((total, width), jnp.bfloat16),
-            pltpu.VMEM((total, 2 * hidden), jnp.bfloat16),
-            pltpu.VMEM((2 * hidden, total), jnp.bfloat16),
-            pltpu.VMEM((hidden, width), jnp.bfloat16),
-            pltpu.VMEM((8, 2, block, width), jnp.bfloat16),
-            pltpu.VMEM((8, block, width), jnp.bfloat16),
-            pltpu.VMEM((4, block, width), jnp.bfloat16),
-            pltpu.VMEM((2, block, width), jnp.bfloat16),
-            pltpu.VMEM((block, width), jnp.bfloat16),
-            dma((4,)), dma((8,)), dma((8,)), dma((12,)), dma((12,)), dma((6,)), dma((6,)), dma((3,)), dma((3,)),
-        ],
+        in_specs=[hbm] * 7,
+        out_specs=out_specs,
+        out_shape=out_shape,
+        scratch_shapes=scratch,
         compiler_params=pltpu.CompilerParams(
             collective_id=layer, has_side_effects=True, vmem_limit_bytes=VMEM_MAX
         ),
@@ -358,7 +477,7 @@
             flops=6 * total * hidden * width * 5, bytes_accessed=8 * hidden * width, transcendentals=0
         ),
         name=f"lstm_grads_{layer}",
-    )(dz, x_rows, h_all, w_stack)
+    )(dz, db, x_rows, h_all, w_stack, gates, c_all)
 
 
 def widen_kernel(part_ref, *refs):
@@ -394,15 +513,18 @@
         db_list = []
         dw_sum = None
         waiting = None
+        dz, db = backward(layers - 1, e_rows, w_stack, gates, c_all, rows)
         for layer in reversed(range(layers)):
-            dz, db = backward(layer, e_rows, w_stack, gates, c_all, rows)
-            db_list.append(jnp.sum(db, axis=0))
-            shard, e_rows = grads(layer, dz, x_rows, h_all, w_stack, rows)
+            shard, db_sum, *rest = grads(layer, dz, db, x_rows, h_all, w_stack, gates, c_all, rows)
+            if layer:
+                dz, db = rest
+            db_list.append(db_sum)
             if waiting is not None:
                 summed, shard = lax.optimization_barrier((waiting, shard))
                 dw_sum = widen(dw_sum, summed, layer + 1, layers)
             waiting = lax.all_gather(shard, batch_axes, axis=0, tiled=True)
-        db_sum = lax.psum(jnp.stack(db_list[::-1]).astype(jnp.bfloat16), batch_axes).astype(jnp.float32)
+        e_rows = rest[0]
+        db_sum = jnp.concatenate(db_list[::-1], axis=0)
         dw_sum = widen(dw_sum, waiting, 0, layers)
         dx = jnp.swapaxes(e_rows.reshape(steps, rows, hidden), 0, 1)
         return dw_sum, db_sum, dx

time: 768 us -> 752 us (0.979)
  blocking collectives: 32.7 us -> 0 us
  waiting for transfers between devices: 0.13 us -> 23.3 us
    pallas_call x4 -> x1, Pallas kernels: 144 us -> 36 us  [backward(): pl.pallas_call(functools.partial(backward_kernel, rows, steps, hidden), g...]
    pallas_call x4, Pallas kernels: 347 us -> 451 us  [grads(): pl.pallas_call(functools.partial(grads_kernel, layer, rows, hidden), in_s...]
    psum x1 -> x0, blocking collectives: 32.7 us -> none  [local_grads(): lax.psum(jnp.stack(db_list[::-1]).astype(jnp.bfloat16), batch_axes)]
    all_gather x4, waiting for transfers between devices: 0.06 us -> 23.2 us  [local_grads(): waiting = lax.all_gather(shard, batch_axes, axis=0, tiled=True)]
  transfers between devices with their start and end apart: 4 -> 4, of which waited for: 0 -> 2; matrix products, arithmetic and copies ran while one was open for 1% -> 1% of each run, Pallas kernels for 58% -> 55%
where the time goes in v2:
time: 752 us; the launch traced here: 751 us
  Pallas kernels  701 us (93%)
  waiting for transfers between devices  23.3 us (3%)
  between operations  13.8 us (2%)
  local copies, waits for them, and re-layouts  11 us (1%)
    pallas_call x4, Pallas kernels, grads(): pl.pallas_call(functools.partial(grads_kernel, layer, rows, hidden), in_s...  451 us
    pallas_call x1, Pallas kernels, forward(): pl.pallas_call(functools.partial(forward_kernel, rows, steps, hidden), gr...  140 us
    pallas_call x4, Pallas kernels, widen(): pl.pallas_call(widen_kernel, grid=(height // block,), in_specs=[pl.BlockS...  73.1 us
    pallas_call x1, Pallas kernels, backward(): pl.pallas_call(functools.partial(backward_kernel, rows, steps, hidden), g...  36 us
    all_gather x4, waiting for transfers between devices, local_grads(): waiting = lax.all_gather(shard, batch_axes, axis=0, tiled=True)  23.2 us
  transfers between devices with their start and end apart: 4, of which 2 were waited for; matrix products, arithmetic and copies ran while one was open for 1% of the time, Pallas kernels for 55%

profile of v2, /device:TPU:0, one launch (start us, length us, event | category | flops | bytes accessed | tf_op | source)
XLA Modules:
  0.0 751.0 jit_solution(2665744590422360522)
XLA Ops:
  7.2 0.0 all-gather.5.cloned.1.call-start
  7.2 2.8 copy.11
  10.0 4.1 copy.10
  14.1 140.3 %lstm_forward.1 = (bf16[4,544,1024]{2,1,0:T(8,128)(2,1)}, f32[4,512,4096]{2,1,0:T(8,128)}, f32[4,544,1024]{2,1,0:T(8,128)}) custom-call(bf16[512,1024]{1,0:T(8,128)(2,1)} %bitcast.13, bf16[4,2048,4096]{2,1,0:T(8,128)(2,1)} %w_hbm.7, f32[4,4096]{1,0:T(4,128)} %b_ref.1), custom_call_target="tpu_custom_call" | custom-call | flops 34359738368 | bytes 75497472 | tf_op jit(solution)/shard_map/lstm_forward/pallas_call | solution.py:59
  154.4 36.0 %lstm_backward_3.1 = (bf16[512,4096]{1,0:T(8,128)(2,1)}, f32[8,4096]{1,0:T(8,128)}) custom-call(f32[512,1024]{1,0:T(8,128)} %bitcast.11, bf16[4,2048,4096]{2,1,0:T(8,128)(2,1)} %w_hbm.7, f32[4,512,4096]{2,1,0:T(8,128)} %get-tuple-element.29.gates_ref.gates_hbm, f32[4,544,1024]{2,1,0:T(8,128)} %get-tuple-element.30.c_ref.c_hbm), custom_call_target="tpu_custom_call" | custom-call | flops 85899345920 | bytes 23068672 | tf_op jit(solution)/shard_map/lstm_backward_3/pallas_call | solution.py:150
  190.4 92.9 %lstm_grads_3.1 = (bf16[128,4096]{1,0:T(8,128)(2,1)}, f32[1,4096]{1,0:T(1,128)}, bf16[512,4096]{1,0:T(8,128)(2,1)}, f32[8,4096]{1,0:T(8,128)}) custom-call(bf16[512,4096]{1,0:T(8,128)(2,1)} %get-tuple-element.31.dz_hbm, f32[8,4096]{1,0:T(8,128)} %get-tuple-element.32.db_hbm, bf16[512,1024]{1,0:T(8,128)(2,1)} %bitcast.14, ...), custom_call_target="tpu_custom_call" | custom-call | flops 64424509440 | bytes 33554432 | tf_op jit(solution)/shard_map/lstm_grads_3/pallas_call | solution.py:467
  283.4 0.0 all-gather.5.cloned.1.call-update
  283.4 0.2 all-gather.7.cloned.1.call-start
  283.6 121.2 %lstm_grads_2.1 = (bf16[128,4096]{1,0:T(8,128)(2,1)}, f32[1,4096]{1,0:T(1,128)}, bf16[512,4096]{1,0:T(8,128)(2,1)}, f32[8,4096]{1,0:T(8,128)}) custom-call(bf16[512,4096]{1,0:T(8,128)(2,1)} %get-tuple-element.35.dz_hbm, f32[8,4096]{1,0:T(8,128)} %get-tuple-element.36.db_hbm, bf16[512,1024]{1,0:T(8,128)(2,1)} %bitcast.15, ...), custom_call_target="tpu_custom_call" | custom-call | flops 64424509440 | bytes 33554432 | tf_op jit(solution)/shard_map/lstm_grads_2/pallas_call | solution.py:467
  404.8 0.0 all-gather.5.cloned.1.call-done.part_ref
  404.8 0.0 all-gather.7.cloned.1.call-update
  404.9 0.3 all-gather.9.cloned.1.call-start
  405.1 122.0 %lstm_grads_1.1 = (bf16[128,4096]{1,0:T(8,128)(2,1)}, f32[1,4096]{1,0:T(1,128)}, bf16[512,4096]{1,0:T(8,128)(2,1)}, f32[8,4096]{1,0:T(8,128)}) custom-call(bf16[512,4096]{1,0:T(8,128)(2,1)} %get-tuple-element.39.dz_hbm, f32[8,4096]{1,0:T(8,128)} %get-tuple-element.40.db_hbm, bf16[512,1024]{1,0:T(8,128)(2,1)} %bitcast.16, ...), custom_call_target="tpu_custom_call" | custom-call | flops 64424509440 | bytes 33554432 | tf_op jit(solution)/shard_map/lstm_grads_1/pallas_call | solution.py:467
  527.1 0.0 all-gather.7.cloned.1.call-done.part_ref
  527.1 0.0 all-gather.9.cloned.1.call-update
  527.2 0.3 all-gather.11.cloned.1.call-start
  527.5 115.0 %lstm_grads_0.1 = (bf16[128,4096]{1,0:T(8,128)(2,1)}, f32[1,4096]{1,0:T(1,128)}, f32[512,1024]{1,0:T(8,128)}) custom-call(bf16[512,4096]{1,0:T(8,128)(2,1)} %get-tuple-element.43.dz_hbm, f32[8,4096]{1,0:T(8,128)} %get-tuple-element.44.db_hbm, bf16[512,1024]{1,0:T(8,128)(2,1)} %bitcast.17, bf16[4,544,1024]{2,1,0:T(8,128)(2,1)} %get-tuple-element.33.h_hbm, ...), custom_call_target="tpu_custom_call" | custom-call | flops 64424509440 | bytes 33554432 | tf_op jit(solution)/shard_map/lstm_grads_0/pallas_call | solution.py:467
  642.5 6.4 all-gather.9.cloned.1.call-done.part_ref
  648.9 0.0 all-gather.11.cloned.1.call-update
  648.9 4.1 copy.14
  653.0 1.5 pad_maximum_fusion
  654.5 18.3 %widen_3.1.refs_0_ = f32[4,2048,4096]{2,1,0:T(8,128)} custom-call(bf16[2048,4096]{1,0:T(8,128)(2,1)} %all-gather.5.cloned.1.call-done.part_ref), custom_call_target="tpu_custom_call" | custom-call | flops 8388608 | bytes 50331648 | tf_op jit(solution)/shard_map/widen_3/pallas_call | solution.py:490
  672.8 18.3 %widen_2.1.refs_0_ = f32[4,2048,4096]{2,1,0:T(8,128)} custom-call(bf16[2048,4096]{1,0:T(8,128)(2,1)} %all-gather.7.cloned.1.call-done.part_ref, f32[4,2048,4096]{2,1,0:T(8,128)} %widen_3.1.refs_0_), custom_call_target="tpu_custom_call", output_to_operand_aliasing={{}: (1, {})} | custom-call | flops 8388608 | bytes 50331648 | tf_op jit(solution)/shard_map/widen_2/pallas_call | solution.py:490
  691.1 18.3 %widen_1.1.refs_0_ = f32[4,2048,4096]{2,1,0:T(8,128)} custom-call(bf16[2048,4096]{1,0:T(8,128)(2,1)} %all-gather.9.cloned.1.call-done.part_ref, f32[4,2048,4096]{2,1,0:T(8,128)} %widen_2.1.refs_0_), custom_call_target="tpu_custom_call", output_to_operand_aliasing={{}: (1, {})} | custom-call | flops 8388608 | bytes 50331648 | tf_op jit(solution)/shard_map/widen_1/pallas_call | solution.py:490
  709.3 16.8 %all-gather.11.cloned.1.call-done.part_ref = bf16[2048,4096]{1,0:T(8,128)(2,1)} async-done(((bf16[128,4096]{1,0:T(8,128)(2,1)}), bf16[2048,4096]{1,0:T(8,128)(2,1)}) %all-gather.11.cloned.1.call-update) | async-done | bytes 16777232 | tf_op jit(solution)/shard_map/all_gather | solution.py:525
  726.2 18.3 %widen_0.1 = f32[4,2048,4096]{2,1,0:T(8,128)} custom-call(bf16[2048,4096]{1,0:T(8,128)(2,1)} %all-gather.11.cloned.1.call-done.part_ref, f32[4,2048,4096]{2,1,0:T(8,128)} %widen_1.1.refs_0_), custom_call_target="tpu_custom_call", output_to_operand_aliasing={{}: (1, {})} | custom-call | flops 8388608 | bytes 50331648 | tf_op jit(solution)/shard_map/widen_0/pallas_call | solution.py:490
Async XLA Ops:
  7.2 397.7 %all-gather.5.cloned.1.call-start = ((), (), s32[]{:S(2)}) async-start(), calls=%async_computation | async-start | bytes 17825792 | tf_op jit(solution)/shard_map/all_gather | solution.py:525
  283.4 243.7 %all-gather.7.cloned.1.call-start = ((), (), s32[]{:S(2)}) async-start(), calls=%async_computation.1 | async-start | bytes 17825792 | tf_op jit(solution)/shard_map/all_gather | solution.py:525
  404.9 244.0 %all-gather.9.cloned.1.call-start = ((), (), s32[]{:S(2)}) async-start(), calls=%async_computation.2 | async-start | bytes 17825792 | tf_op jit(solution)/shard_map/all_gather | solution.py:525
  527.2 199.0 %all-gather.11.cloned.1.call-start = ((), (), s32[]{:S(2)}) async-start(), calls=%async_computation.3 | async-start | bytes 17825792 | tf_op jit(solution)/shard_map/all_gather | solution.py:525
Sparse Core Ops, SparseCore 0:
  283.5 112.6 all-gather.4
  405.0 113.3 all-gather.6
  527.3 121.5 all-gather.8
  651.0 75.1 all-gather.10

commit v3 on v2

--- a/solution.py
+++ b/solution.py
@@ -15,66 +15,168 @@
     return 0.5 * jnp.tanh(0.5 * z) + 0.5
 
 
-def forward_kernel(rows, steps, hidden, x_ref, w_ref, b_ref, h_ref, gates_ref, c_ref, u_ref):
-    @pl.when(pl.program_id(0) == 0)
-    def _():
-        u_ref[...] = x_ref[...]
-
-    h_ref[0, :rows, :] = jnp.zeros((rows, hidden), jnp.bfloat16)
-    c_ref[0, :rows, :] = jnp.zeros((rows, hidden), jnp.float32)
-
-    @pl.loop(0, 4 * hidden // BLK)
-    def _(n):
-        cols = pl.ds(pl.multiple_of(n * BLK, BLK), BLK)
-        part = jnp.dot(u_ref[...], w_ref[0, :hidden, cols], preferred_element_type=jnp.float32)
-        gates_ref[0, :, cols] = part + b_ref[pl.ds(pl.program_id(0), 1), cols]
-
-    @pl.loop(0, steps)
-    def _(t):
+def forward_kernel(
+    rows, x_hbm, w_hbm, b_ref, h_out, gates_out, c_out,
+    h, gates, c, w_in, w_rec, x_sem, first_sem, in_sem, rec_sem, store_sem,
+):
+    layers, width = b_ref.shape
+    hidden = width // 4
+    total = gates.shape[1]
+    steps = total // rows
+    span = total // 4
+    group = steps // 4
+
+    def load_in(l, slot):
+        return pltpu.make_async_copy(w_hbm.at[l, pl.ds(0, hidden), :], w_in.at[slot], in_sem.at[slot])
+
+    def load_rec(l, slot):
+        return pltpu.make_async_copy(w_hbm.at[l, pl.ds(hidden, hidden), :], w_rec.at[slot], rec_sem.at[slot])
+
+    def load_first(k):
+        cols = pl.ds(k * hidden, hidden)
+        return pltpu.make_async_copy(w_hbm.at[0, pl.ds(0, hidden), cols], w_in.at[0, :, cols], first_sem.at[k])
+
+    def stores(l, slot, t):
         now = pl.ds(pl.multiple_of(t * rows, rows), rows)
         later = pl.ds(pl.multiple_of(t * rows + rows, rows), rows)
-        h_prev = h_ref[0, now, :]
-        for j in range(hidden // BLK):
-            cols = [pl.ds(k * hidden + j * BLK, BLK) for k in range(4)]
-            z = [
-                gates_ref[0, now, col] + jnp.dot(h_prev, w_ref[0, hidden:, col], preferred_element_type=jnp.float32)
-                for col in cols
-            ]
-            act = [sigmoid(z[0]), sigmoid(z[1]), jnp.tanh(z[2]), sigmoid(z[3])]
-            for col, value in zip(cols, act):
-                gates_ref[0, now, col] = value
-            part = pl.ds(j * BLK, BLK)
-            c_new = act[1] * c_ref[0, now, part] + act[0] * act[2]
-            c_ref[0, later, part] = c_new
-            h_ref[0, later, part] = (act[3] * jnp.tanh(c_new)).astype(jnp.bfloat16)
-
-    u_ref[...] = h_ref[0, rows:, :]
+        return [
+            pltpu.make_async_copy(gates.at[slot, now, :], gates_out.at[l, now, :], store_sem.at[slot, 0]),
+            pltpu.make_async_copy(h.at[slot, later, :], h_out.at[l, later, :], store_sem.at[slot, 1]),
+            pltpu.make_async_copy(c.at[slot, later, :], c_out.at[l, later, :], store_sem.at[slot, 2]),
+        ]
+
+    def zero_stores(l, slot):
+        at = pl.ds(0, rows)
+        return [
+            pltpu.make_async_copy(h.at[slot, at, :], h_out.at[l, at, :], store_sem.at[slot, 1]),
+            pltpu.make_async_copy(c.at[slot, at, :], c_out.at[l, at, :], store_sem.at[slot, 2]),
+        ]
+
+    def finish_stores(l, slot):
+        for copy in zero_stores(l, slot):
+            copy.wait()
+
+        @pl.loop(0, steps)
+        def _(t):
+            for copy in stores(l, slot, t):
+                copy.wait()
+
+    x_load = pltpu.make_async_copy(x_hbm, h.at[1, pl.ds(rows, total), :], x_sem)
+    x_load.start()
+    for k in range(4):
+        load_first(k).start()
+    load_rec(0, 0).start()
+    load_in(1, 1).start()
+    for slot in range(2):
+        h[slot, :rows, :] = jnp.zeros((rows, hidden), jnp.bfloat16)
+        c[slot, :rows, :] = jnp.zeros((rows, hidden), jnp.float32)
+    x_load.wait()
+    for k in range(4):
+        load_first(k).wait()
+
+        @pl.loop(0, hidden // BLK)
+        def _(n):
+            cols = pl.ds(pl.multiple_of(k * hidden + n * BLK, BLK), BLK)
+            part = jnp.dot(h[1, rows : rows + 3 * span, :], w_in[0, :, cols], preferred_element_type=jnp.float32)
+            gates[0, : 3 * span, cols] = part + b_ref[0:1, cols]
+
+    @pl.loop(0, layers)
+    def _(l):
+        slot = lax.rem(l, 2)
+        other = 1 - slot
+
+        @pl.when(l + 1 < layers)
+        def _():
+            load_rec(l + 1, other).start()
+
+        for copy in zero_stores(l, slot):
+            copy.start()
+        load_rec(l, slot).wait()
+
+        @pl.when((l > 0) & (l + 1 < layers))
+        def _():
+            load_in(l + 1, other).wait()
+
+        @pl.when(l == 0)
+        def _():
+            load_in(1, 1).wait()
+
+        @pl.loop(0, steps)
+        def _(t):
+            now = pl.ds(pl.multiple_of(t * rows, rows), rows)
+            later = pl.ds(pl.multiple_of(t * rows + rows, rows), rows)
+            h_prev = h[slot, now, :]
+            for j in range(hidden // BLK):
+                cols = [pl.ds(k * hidden + j * BLK, BLK) for k in range(4)]
+                z = [
+                    gates[slot, now, col]
+                    + jnp.dot(h_prev, w_rec[slot, :, col], preferred_element_type=jnp.float32)
+                    for col in cols
+                ]
+                if j == hidden // BLK - 1:
+                    early = t < group
+                    source = jnp.where(early, other, slot)
+                    target = jnp.where(early, slot, other)
+                    row = pl.multiple_of(jnp.where(early, 3, t // group - 1) * span, span)
+                    bias = jnp.minimum(jnp.where(early, l, l + 1), layers - 1)
+                    u = h[source, pl.ds(pl.multiple_of(row + rows, rows), span), :]
+                    for i in range(width // group // BLK):
+                        col = pl.ds(pl.multiple_of(lax.rem(t, group) * (width // group) + i * BLK, BLK), BLK)
+                        gates[target, pl.ds(row, span), col] = b_ref[pl.ds(bias, 1), col] + jnp.dot(
+                            u, w_in[target, :, col], preferred_element_type=jnp.float32
+                        )
+                act = [sigmoid(z[0]), sigmoid(z[1]), jnp.tanh(z[2]), sigmoid(z[3])]
+                for col, value in zip(cols, act):
+                    gates[slot, now, col] = value
+                part = pl.ds(j * BLK, BLK)
+                c_new = act[1] * c[slot, now, part] + act[0] * act[2]
+                c[slot, later, part] = c_new
+                h[slot, later, part] = (act[3] * jnp.tanh(c_new)).astype(jnp.bfloat16)
+
+            @pl.when(t > 0)
+            def _():
+                for copy in stores(l, slot, t - 1):
+                    copy.start()
+
+            @pl.when(t == group - 1)
+            def _():
+                @pl.when(l > 0)
+                def _():
+                    finish_stores(l - 1, other)
+
+                @pl.when(l + 2 < layers)
+                def _():
+                    load_in(l + 2, slot).start()
+
+        for copy in stores(l, slot, steps - 1):
+            copy.start()
+
+    finish_stores(layers - 1, (layers - 1) % 2)
 
 
 def forward(x_rows, w_stack, b_stack, rows):
     layers, _, width = w_stack.shape
     hidden = width // 4
     total = x_rows.shape[0]
-    steps = total // rows
+    dma = pltpu.SemaphoreType.DMA
+    hbm = pl.BlockSpec(memory_space=pl.ANY)
     return pl.pallas_call(
-        functools.partial(forward_kernel, rows, steps, hidden),
-        grid=(layers,),
-        in_specs=[
-            pl.BlockSpec((total, hidden), lambda l: (0, 0)),
-            pl.BlockSpec((1, 2 * hidden, width), lambda l: (l, 0, 0)),
-            pl.BlockSpec((layers, width), lambda l: (0, 0)),
-        ],
-        out_specs=[
-            pl.BlockSpec((1, total + rows, hidden), lambda l: (l, 0, 0)),
-            pl.BlockSpec((1, total, width), lambda l: (l, 0, 0)),
-            pl.BlockSpec((1, total + rows, hidden), lambda l: (l, 0, 0)),
-        ],
+        functools.partial(forward_kernel, rows),
+        in_specs=[hbm, hbm, pl.BlockSpec(memory_space=pltpu.VMEM)],
+        out_specs=[hbm] * 3,
         out_shape=[
             jax.ShapeDtypeStruct((layers, total + rows, hidden), jnp.bfloat16),
             jax.ShapeDtypeStruct((layers, total, width), jnp.float32),
             jax.ShapeDtypeStruct((layers, total + rows, hidden), jnp.float32),
         ],
-        scratch_shapes=[pltpu.VMEM((total, hidden), jnp.bfloat16)],
+        scratch_shapes=[
+            pltpu.VMEM((2, total + rows, hidden), jnp.bfloat16),
+            pltpu.VMEM((2, total, width), jnp.float32),
+            pltpu.VMEM((2, total + rows, hidden), jnp.float32),
+            pltpu.VMEM((2, hidden, width), jnp.bfloat16),
+            pltpu.VMEM((2, hidden, width), jnp.bfloat16),
+            dma, dma((4,)), dma((2,)), dma((2,)), dma((2, 3)),
+        ],
         compiler_params=pltpu.CompilerParams(vmem_limit_bytes=VMEM_MAX),
         cost_estimate=pl.CostEstimate(
             flops=2 * layers * total * 2 * hidden * width,
@@ -85,7 +187,7 @@
     )(x_rows, w_stack, b_stack)
 
 
-def backward_step(rows, hidden, t, gate, e_ref, c, wt_ref, r_ref, dc_ref, dz_ref, db_ref):
+def backward_step(rows, hidden, t, gate, e, c, wt_ref, r_ref, dc_ref, dz_ref, db_ref):
     now = pl.ds(pl.multiple_of(t * rows, rows), rows)
     later = pl.ds(pl.multiple_of(t * rows + rows, rows), rows)
     total = None
@@ -94,7 +196,7 @@
         cols = [pl.ds(k * hidden + j * BLK, BLK) for k in range(4)]
         gate_i, gate_f, gate_g, gate_o = [gate(col) for col in cols]
         tanh_c = jnp.tanh(c(later, part))
-        dh = e_ref[now, part] + r_ref[:, part]
+        dh = e(part) + r_ref[:, part]
         dc = dc_ref[:, part] + dh * gate_o * (1.0 - tanh_c * tanh_c)
         dz = [
             dc * gate_g * gate_i * (1.0 - gate_i),
@@ -117,29 +219,79 @@
     r_ref[...] = total
 
 
-def transpose_recurrent(hidden, w, wt_ref):
+def transpose_gate(hidden, k, w_ref, wt_ref):
     @pl.loop(0, hidden // BLK)
     def _(j):
-        for k in range(4):
-            cols = pl.ds(pl.multiple_of(k * hidden + j * BLK, BLK), BLK)
-            place = pl.ds(pl.multiple_of(j * 4 * BLK + k * BLK, BLK), BLK)
-            wt_ref[place, :] = w(cols).T
-
-
-def backward_kernel(rows, steps, hidden, e_ref, w_ref, gates_ref, c_ref, dz_ref, db_ref, wt_ref, r_ref, dc_ref):
-    transpose_recurrent(hidden, lambda cols: w_ref[0, :, cols], wt_ref)
+        cols = pl.ds(pl.multiple_of(k * hidden + j * BLK, BLK), BLK)
+        place = pl.ds(pl.multiple_of(j * 4 * BLK + k * BLK, BLK), BLK)
+        wt_ref[place, :] = w_ref[:, cols].T
+
+
+def backward_kernel(
+    layer, rows, steps, hidden, e_hbm, w_hbm, gates_hbm, c_hbm, dz_out, db_ref,
+    e_all, w, c_all, ring, dz, wt_ref, r_ref, dc_ref, w_sem, ring_sem, out_sem, sem,
+):
+    depth = ring.shape[0]
+
+    def gates_load(s, slot):
+        at = pl.ds(pl.multiple_of((steps - 1 - s) * rows, rows), rows)
+        return pltpu.make_async_copy(gates_hbm.at[layer, at, :], ring.at[slot], ring_sem.at[slot])
+
+    def store(s):
+        at = pl.ds(pl.multiple_of((steps - 1 - s) * rows, rows), rows)
+        return pltpu.make_async_copy(dz.at[at, :], dz_out.at[at, :], out_sem)
+
+    def e_step(t, col):
+        first, count = col.start // 128, col.size // 128
+        at = pl.ds(t, rows, stride=steps)
+        return jnp.concatenate([e_all[first + i, at, :] for i in range(count)], axis=1)
+
+    def w_load(k):
+        cols = pl.ds(k * hidden, hidden)
+        return pltpu.make_async_copy(w_hbm.at[layer, pl.ds(hidden, hidden), cols], w.at[:, cols], w_sem.at[k])
+
+    tiles = hidden // 128
+    loads = [pltpu.make_async_copy(c_hbm.at[layer], c_all, sem.at[tiles])]
+    for i in range(tiles):
+        loads.append(pltpu.make_async_copy(e_hbm.at[:, pl.ds(i * 128, 128)], e_all.at[i], sem.at[i]))
+    for k in range(4):
+        w_load(k).start()
+    for load in loads:
+        load.start()
+    for s in range(min(depth, steps)):
+        gates_load(s, s).start()
     r_ref[...] = jnp.zeros_like(r_ref)
     dc_ref[...] = jnp.zeros_like(dc_ref)
     db_ref[...] = jnp.zeros_like(db_ref)
+    for k in range(4):
+        w_load(k).wait()
+        transpose_gate(hidden, k, w, wt_ref)
+    for load in loads:
+        load.wait()
 
     @pl.loop(0, steps)
     def _(s):
         t = steps - 1 - s
-        now = pl.ds(pl.multiple_of(t * rows, rows), rows)
+        slot = lax.rem(s, depth)
+        gates_load(s, slot).wait()
         backward_step(
-            rows, hidden, t, lambda col: gates_ref[0, now, col], e_ref, lambda at, col: c_ref[0, at, col],
-            wt_ref, r_ref, dc_ref, dz_ref, db_ref,
+            rows, hidden, t, lambda col: ring[slot, :, col], lambda col: e_step(t, col),
+            lambda at, col: c_all[at, col], wt_ref, r_ref, dc_ref, dz, db_ref,
         )
+
+        @pl.when(s + depth < steps)
+        def _():
+            gates_load(s + depth, slot).start()
+
+        @pl.when(s > 0)
+        def _():
+            store(s - 1).start()
+
+    store(steps - 1).start()
+
+    @pl.loop(0, steps)
+    def _(s):
+        store(s).wait()
 
 
 def backward(layer, e_rows, w_stack, gates, c_all, rows):
@@ -147,27 +299,25 @@
     hidden = width // 4
     total = e_rows.shape[0]
     steps = total // rows
+    dma = pltpu.SemaphoreType.DMA
     return pl.pallas_call(
-        functools.partial(backward_kernel, rows, steps, hidden),
-        grid=(1,),
-        in_specs=[
-            pl.BlockSpec((total, hidden), lambda i: (0, 0), pipeline_mode=pl.Buffered(1)),
-            pl.BlockSpec((1, hidden, width), lambda i: (layer, 1, 0), pipeline_mode=pl.Buffered(1)),
-            pl.BlockSpec((1, total, width), lambda i: (layer, 0, 0), pipeline_mode=pl.Buffered(1)),
-            pl.BlockSpec((1, total + rows, hidden), lambda i: (layer, 0, 0), pipeline_mode=pl.Buffered(1)),
-        ],
-        out_specs=[
-            pl.BlockSpec((total, width), lambda i: (0, 0), pipeline_mode=pl.Buffered(1)),
-            pl.BlockSpec((8, width), lambda i: (0, 0), pipeline_mode=pl.Buffered(1)),
-        ],
+        functools.partial(backward_kernel, layer, rows, steps, hidden),
+        in_specs=[pl.BlockSpec(memory_space=pl.ANY)] * 4,
+        out_specs=[pl.BlockSpec(memory_space=pl.ANY), pl.BlockSpec(memory_space=pltpu.VMEM)],
         out_shape=[
             jax.ShapeDtypeStruct((total, width), jnp.bfloat16),
             jax.ShapeDtypeStruct((8, width), jnp.float32),
         ],
         scratch_shapes=[
+            pltpu.VMEM((hidden // 128, total, 128), jnp.float32),
+            pltpu.VMEM((hidden, width), jnp.bfloat16),
+            pltpu.VMEM((total + rows, hidden), jnp.float32),
+            pltpu.VMEM((4, rows, width), jnp.float32),
+            pltpu.VMEM((total, width), jnp.bfloat16),
             pltpu.VMEM((width, hidden), jnp.bfloat16),
             pltpu.VMEM((rows, hidden), jnp.float32),
             pltpu.VMEM((rows, hidden), jnp.float32),
+            dma((4,)), dma((4,)), dma, dma((hidden // 128 + 1,)),
         ],
         compiler_params=pltpu.CompilerParams(vmem_limit_bytes=VMEM_MAX),
         cost_estimate=pl.CostEstimate(
@@ -362,6 +512,15 @@
                     if (here >> axes[1]) & 1:
                         copies[2, k, (here >> axes[2]) & 1].start()
 
+    def second_crossing(bit):
+        for k, axes in enumerate(AXES):
+            cols = pl.ds(*columns[k])
+            copies[2, k, bit].wait_recv()
+            mine = p.at[bit << axes[2], c, :, cols]
+            add_into(mine, mine, r2.at[bit, :, cols])
+            if bit:
+                copies[3, k].start()
+
     bias_stage(1)
     if layer:
         reload = pltpu.make_async_copy(w_hbm.at[below, pl.ds(hidden, hidden), :], w, local_sem.at[4])
@@ -371,14 +530,18 @@
         db_ref[...] = jnp.zeros_like(db_ref)
         loads[5].wait()
         reload.wait()
-        transpose_recurrent(hidden, lambda cols: w[:, cols], r0)
+        first_crossing(ORDER[:1])
+        for k in range(4):
+            transpose_gate(hidden, k, w, r0)
 
         @pl.loop(0, steps)
         def _(s):
+            t = steps - 1 - s
             slot = lax.rem(s, depth)
             gates_load(s, slot).wait()
+            now = pl.ds(pl.multiple_of(t * rows, rows), rows)
             backward_step(
-                rows, hidden, steps - 1 - s, lambda col: ring[slot, :, col], dx_ref,
+                rows, hidden, t, lambda col: ring[slot, :, col], lambda col: dx_ref[now, col],
                 lambda at, col: c_all[at, col], r0, r_ref, dc_ref, dz, db_ref,
             )
 
@@ -386,28 +549,29 @@
             def _():
                 gates_load(s + depth, slot).start()
 
-            @pl.when(s == steps // 2 - 2)
+            @pl.when(s == steps // 16)
             def _():
-                first_crossing(ORDER[:1])
+                first_crossing(ORDER[1:4])
+
+            @pl.when(s == steps // 4)
+            def _():
+                first_crossing(ORDER[4:])
+
+            @pl.when(s == steps // 2)
+            def _():
+                second_crossing(1)
 
             @pl.when(s == steps - 3)
             def _():
-                first_crossing(ORDER[1:4])
+                second_crossing(0)
 
         store = pltpu.make_async_copy(dz, dz_out, local_sem.at[2])
         store.start()
-        first_crossing(ORDER[4:])
     else:
         first_crossing(ORDER)
+        second_crossing(1)
+        second_crossing(0)
     bias_stage(2)
-    for bit in (1, 0):
-        for k, axes in enumerate(AXES):
-            cols = pl.ds(*columns[k])
-            copies[2, k, bit].wait_recv()
-            mine = p.at[bit << axes[2], c, :, cols]
-            add_into(mine, mine, r2.at[bit, :, cols])
-            if bit:
-                copies[3, k].start()
     bias_stage(3)
     for k in range(3):
         cols = pl.ds(*columns[k])
@@ -508,7 +672,7 @@
         hidden = width // 4
         rows, steps, _ = x_loc.shape
         x_rows = jnp.swapaxes(x_loc, 0, 1).reshape(steps * rows, hidden)
-        e_rows = jnp.swapaxes(dy_loc, 0, 1).reshape(steps * rows, hidden)
+        e_rows = dy_loc.reshape(rows * steps, hidden)
         h_all, gates, c_all = forward(x_rows, w_stack, b_stack, rows)
         db_list = []
         dw_sum = None
@@ -525,6 +689,7 @@
             waiting = lax.all_gather(shard, batch_axes, axis=0, tiled=True)
         e_rows = rest[0]
         db_sum = jnp.concatenate(db_list[::-1], axis=0)
+        waiting, dw_sum = lax.optimization_barrier((waiting, dw_sum))
         dw_sum = widen(dw_sum, waiting, 0, layers)
         dx = jnp.swapaxes(e_rows.reshape(steps, rows, hidden), 0, 1)
         return dw_sum, db_sum, dx

time: 752 us -> 734 us (0.976)
  Pallas kernels: 701 us -> 675 us
  waiting for transfers between devices: 23.3 us -> 34.7 us
    pallas_call x4, Pallas kernels: 451 us -> 434 us  [grads(): pl.pallas_call(functools.partial(grads_kernel, layer, rows, hidden), in_s...]
    all_gather x4, waiting for transfers between devices: 23.2 us -> 34.6 us  [local_grads(): waiting = lax.all_gather(shard, batch_axes, axis=0, tiled=True)]
    pallas_call x2, Pallas kernels: 176 us -> 167 us  [the longest x1 135 us: forward(): pl.pallas_call(functools.partial(forward_kernel, rows), in_specs=[hbm, hb...]
  transfers between devices with their start and end apart: 4 -> 4, of which waited for: 2 -> 4; matrix products, arithmetic and copies ran while one was open for 1% -> 1% of each run, Pallas kernels for 55% -> 55%
where the time goes in v3:
time: 734 us; the launch traced here: 733 us
  Pallas kernels  675 us (92%)
  waiting for transfers between devices  34.7 us (5%)
  between operations  13.8 us (2%)
    pallas_call x4, Pallas kernels, grads(): pl.pallas_call(functools.partial(grads_kernel, layer, rows, hidden), in_s...  434 us
    pallas_call x1, Pallas kernels, forward(): pl.pallas_call(functools.partial(forward_kernel, rows), in_specs=[hbm, hb...  135 us
    pallas_call x4, Pallas kernels, widen(): pl.pallas_call(widen_kernel, grid=(height // block,), in_specs=[pl.BlockS...  73.1 us
    all_gather x4, waiting for transfers between devices, local_grads(): waiting = lax.all_gather(shard, batch_axes, axis=0, tiled=True)  34.6 us
    pallas_call x1, Pallas kernels, backward(): pl.pallas_call(functools.partial(backward_kernel, layer, rows, steps, hid...  32.1 us
  transfers between devices with their start and end apart: 4, of which 4 were waited for; matrix products, arithmetic and copies ran while one was open for 1% of the time, Pallas kernels for 55%

profile of v3, /device:TPU:0, one launch (start us, length us, event | category | flops | bytes accessed | tf_op | source)
XLA Modules:
  0.0 732.7 jit_solution(7818185199245670842)
XLA Ops:
  7.2 0.0 all-gather.5.cloned.1.call-start
  7.2 2.8 copy.10
  10.0 135.4 %lstm_forward.1 = (bf16[4,544,1024]{2,1,0:T(8,128)(2,1)}, f32[4,512,4096]{2,1,0:T(8,128)}, f32[4,544,1024]{2,1,0:T(8,128)}) custom-call(bf16[512,1024]{1,0:T(8,128)(2,1)} %bitcast.10, bf16[4,2048,4096]{2,1,0:T(8,128)(2,1)} %w_hbm.11, f32[4,4096]{1,0:T(4,128)} %b_ref.1), custom_call_target="tpu_custom_call" | custom-call | flops 34359738368 | bytes 75497472 | tf_op jit(solution)/shard_map/lstm_forward/pallas_call | solution.py:163
  145.4 32.1 %lstm_backward_3.1 = (bf16[512,4096]{1,0:T(8,128)(2,1)}, f32[8,4096]{1,0:T(8,128)}) custom-call(f32[512,1024]{1,0:T(8,128)} %bitcast.15, bf16[4,2048,4096]{2,1,0:T(8,128)(2,1)} %w_hbm.11, f32[4,512,4096]{2,1,0:T(8,128)} %get-tuple-element.31.gates_hbm, f32[4,544,1024]{2,1,0:T(8,128)} %get-tuple-element.32.c_hbm), custom_call_target="tpu_custom_call" | custom-call | flops 85899345920 | bytes 23068672 | tf_op jit(solution)/shard_map/lstm_backward_3/pallas_call | solution.py:303
  177.5 82.8 %lstm_grads_3.1 = (bf16[128,4096]{1,0:T(8,128)(2,1)}, f32[1,4096]{1,0:T(1,128)}, bf16[512,4096]{1,0:T(8,128)(2,1)}, f32[8,4096]{1,0:T(8,128)}) custom-call(bf16[512,4096]{1,0:T(8,128)(2,1)} %get-tuple-element.33.dz_hbm, f32[8,4096]{1,0:T(8,128)} %get-tuple-element.34.db_hbm, bf16[512,1024]{1,0:T(8,128)(2,1)} %bitcast.11, ...), custom_call_target="tpu_custom_call" | custom-call | flops 64424509440 | bytes 33554432 | tf_op jit(solution)/shard_map/lstm_grads_3/pallas_call | solution.py:631
  260.3 0.0 all-gather.5.cloned.1.call-update
  260.3 0.2 all-gather.7.cloned.1.call-start
  260.5 117.7 %lstm_grads_2.1 = (bf16[128,4096]{1,0:T(8,128)(2,1)}, f32[1,4096]{1,0:T(1,128)}, bf16[512,4096]{1,0:T(8,128)(2,1)}, f32[8,4096]{1,0:T(8,128)}) custom-call(bf16[512,4096]{1,0:T(8,128)(2,1)} %get-tuple-element.37.dz_hbm, f32[8,4096]{1,0:T(8,128)} %get-tuple-element.38.db_hbm, bf16[512,1024]{1,0:T(8,128)(2,1)} %bitcast.12, ...), custom_call_target="tpu_custom_call" | custom-call | flops 64424509440 | bytes 33554432 | tf_op jit(solution)/shard_map/lstm_grads_2/pallas_call | solution.py:631
  378.2 3.8 all-gather.5.cloned.1.call-done.part_ref
  382.0 0.0 all-gather.7.cloned.1.call-update
  382.0 0.3 all-gather.9.cloned.1.call-start
  382.3 119.6 %lstm_grads_1.1 = (bf16[128,4096]{1,0:T(8,128)(2,1)}, f32[1,4096]{1,0:T(1,128)}, bf16[512,4096]{1,0:T(8,128)(2,1)}, f32[8,4096]{1,0:T(8,128)}) custom-call(bf16[512,4096]{1,0:T(8,128)(2,1)} %get-tuple-element.41.dz_hbm, f32[8,4096]{1,0:T(8,128)} %get-tuple-element.42.db_hbm, bf16[512,1024]{1,0:T(8,128)(2,1)} %bitcast.13, ...), custom_call_target="tpu_custom_call" | custom-call | flops 64424509440 | bytes 33554432 | tf_op jit(solution)/shard_map/lstm_grads_1/pallas_call | solution.py:631
  501.9 5.1 all-gather.7.cloned.1.call-done.part_ref
  507.0 0.0 all-gather.9.cloned.1.call-update
  507.1 0.3 all-gather.11.cloned.1.call-start
  507.4 114.3 %lstm_grads_0.1 = (bf16[128,4096]{1,0:T(8,128)(2,1)}, f32[1,4096]{1,0:T(1,128)}, f32[512,1024]{1,0:T(8,128)}) custom-call(bf16[512,4096]{1,0:T(8,128)(2,1)} %get-tuple-element.45.dz_hbm, f32[8,4096]{1,0:T(8,128)} %get-tuple-element.46.db_hbm, bf16[512,1024]{1,0:T(8,128)(2,1)} %bitcast.14, bf16[4,544,1024]{2,1,0:T(8,128)(2,1)} %get-tuple-element.35.h_hbm, ...), custom_call_target="tpu_custom_call" | custom-call | flops 64424509440 | bytes 33554432 | tf_op jit(solution)/shard_map/lstm_grads_0/pallas_call | solution.py:631
  621.7 7.8 %all-gather.9.cloned.1.call-done.part_ref = bf16[2048,4096]{1,0:T(8,128)(2,1)} async-done(((bf16[128,4096]{1,0:T(8,128)(2,1)}), bf16[2048,4096]{1,0:T(8,128)(2,1)}) %all-gather.9.cloned.1.call-update) | async-done | bytes 16777232 | tf_op jit(solution)/shard_map/all_gather | solution.py:689
  629.5 0.0 all-gather.11.cloned.1.call-update
  629.5 4.1 copy.13
  633.6 1.5 pad_maximum_fusion
  635.1 18.3 %widen_3.1.refs_0_ = f32[4,2048,4096]{2,1,0:T(8,128)} custom-call(bf16[2048,4096]{1,0:T(8,128)(2,1)} %all-gather.5.cloned.1.call-done.part_ref), custom_call_target="tpu_custom_call" | custom-call | flops 8388608 | bytes 50331648 | tf_op jit(solution)/shard_map/widen_3/pallas_call | solution.py:654
  653.4 18.3 %widen_2.1.refs_0_ = f32[4,2048,4096]{2,1,0:T(8,128)} custom-call(bf16[2048,4096]{1,0:T(8,128)(2,1)} %all-gather.7.cloned.1.call-done.part_ref, f32[4,2048,4096]{2,1,0:T(8,128)} %widen_3.1.refs_0_), custom_call_target="tpu_custom_call", output_to_operand_aliasing={{}: (1, {})} | custom-call | flops 8388608 | bytes 50331648 | tf_op jit(solution)/shard_map/widen_2/pallas_call | solution.py:654
  671.7 18.3 %widen_1.1.refs_0_ = f32[4,2048,4096]{2,1,0:T(8,128)} custom-call(bf16[2048,4096]{1,0:T(8,128)(2,1)} %all-gather.9.cloned.1.call-done.part_ref, f32[4,2048,4096]{2,1,0:T(8,128)} %widen_2.1.refs_0_), custom_call_target="tpu_custom_call", output_to_operand_aliasing={{}: (1, {})} | custom-call | flops 8388608 | bytes 50331648 | tf_op jit(solution)/shard_map/widen_1/pallas_call | solution.py:654
  690.0 17.9 %all-gather.11.cloned.1.call-done.part_ref = bf16[2048,4096]{1,0:T(8,128)(2,1)} async-done(((bf16[128,4096]{1,0:T(8,128)(2,1)}), bf16[2048,4096]{1,0:T(8,128)(2,1)}) %all-gather.11.cloned.1.call-update) | async-done | bytes 16777232 | tf_op jit(solution)/shard_map/all_gather | solution.py:689
  707.9 18.3 %widen_0.1 = f32[4,2048,4096]{2,1,0:T(8,128)} custom-call(bf16[2048,4096]{1,0:T(8,128)(2,1)} %all-gather.11.cloned.1.call-done.part_ref, f32[4,2048,4096]{2,1,0:T(8,128)} %widen_1.1.refs_0_), custom_call_target="tpu_custom_call", output_to_operand_aliasing={{}: (1, {})} | custom-call | flops 8388608 | bytes 50331648 | tf_op jit(solution)/shard_map/widen_0/pallas_call | solution.py:654
Async XLA Ops:
  7.2 374.8 %all-gather.5.cloned.1.call-start = ((), (), s32[]{:S(2)}) async-start(), calls=%async_computation | async-start | bytes 17825792 | tf_op jit(solution)/shard_map/all_gather | solution.py:689
  260.3 246.8 %all-gather.7.cloned.1.call-start = ((), (), s32[]{:S(2)}) async-start(), calls=%async_computation.1 | async-start | bytes 17825792 | tf_op jit(solution)/shard_map/all_gather | solution.py:689
  382.0 247.5 %all-gather.9.cloned.1.call-start = ((), (), s32[]{:S(2)}) async-start(), calls=%async_computation.2 | async-start | bytes 17825792 | tf_op jit(solution)/shard_map/all_gather | solution.py:689
  507.1 200.8 %all-gather.11.cloned.1.call-start = ((), (), s32[]{:S(2)}) async-start(), calls=%async_computation.3 | async-start | bytes 17825792 | tf_op jit(solution)/shard_map/all_gather | solution.py:689
Sparse Core Ops, SparseCore 0:
  260.4 121.5 all-gather.4
  384.2 122.7 all-gather.6
  509.3 120.1 all-gather.8
  631.6 76.2 all-gather.10

commit v4 on v3

--- a/solution.py
+++ b/solution.py
@@ -9,6 +9,7 @@
 
 VMEM_MAX = 67043328
 BLK = 256
+PAD = 256
 
 
 def sigmoid(z):
@@ -27,10 +28,10 @@
     group = steps // 4
 
     def load_in(l, slot):
-        return pltpu.make_async_copy(w_hbm.at[l, pl.ds(0, hidden), :], w_in.at[slot], in_sem.at[slot])
+        return pltpu.make_async_copy(w_hbm.at[l, pl.ds(0, hidden), :], w_in.at[slot, :, pl.ds(0, width)], in_sem.at[slot])
 
     def load_rec(l, slot):
-        return pltpu.make_async_copy(w_hbm.at[l, pl.ds(hidden, hidden), :], w_rec.at[slot], rec_sem.at[slot])
+        return pltpu.make_async_copy(w_hbm.at[l, pl.ds(hidden, hidden), :], w_rec.at[slot, :, pl.ds(0, width)], rec_sem.at[slot])
 
     def load_first(k):
         cols = pl.ds(k * hidden, hidden)
@@ -173,8 +174,8 @@
             pltpu.VMEM((2, total + rows, hidden), jnp.bfloat16),
             pltpu.VMEM((2, total, width), jnp.float32),
             pltpu.VMEM((2, total + rows, hidden), jnp.float32),
-            pltpu.VMEM((2, hidden, width), jnp.bfloat16),
-            pltpu.VMEM((2, hidden, width), jnp.bfloat16),
+            pltpu.VMEM((2, hidden, width + PAD), jnp.bfloat16),
+            pltpu.VMEM((2, hidden, width + PAD), jnp.bfloat16),
             dma, dma((4,)), dma((2,)), dma((2,)), dma((2, 3)),
         ],
         compiler_params=pltpu.CompilerParams(vmem_limit_bytes=VMEM_MAX),
@@ -212,7 +213,7 @@
             db_ref[:, col] += jnp.sum(value.reshape(rows // 8, 8, BLK), axis=0)
         back = jnp.dot(
             jnp.concatenate(low, axis=1),
-            wt_ref[j * 4 * BLK : (j + 1) * 4 * BLK, :],
+            wt_ref[j * 4 * BLK : (j + 1) * 4 * BLK, :hidden],
             preferred_element_type=jnp.float32,
         )
         total = back if total is None else total + back
@@ -224,7 +225,7 @@
     def _(j):
         cols = pl.ds(pl.multiple_of(k * hidden + j * BLK, BLK), BLK)
         place = pl.ds(pl.multiple_of(j * 4 * BLK + k * BLK, BLK), BLK)
-        wt_ref[place, :] = w_ref[:, cols].T
+        wt_ref[place, :hidden] = w_ref[:, cols].T
 
 
 def backward_kernel(
@@ -314,7 +315,7 @@
             pltpu.VMEM((total + rows, hidden), jnp.float32),
             pltpu.VMEM((4, rows, width), jnp.float32),
             pltpu.VMEM((total, width), jnp.bfloat16),
-            pltpu.VMEM((width, hidden), jnp.bfloat16),
+            pltpu.VMEM((width, hidden + PAD), jnp.bfloat16),
             pltpu.VMEM((rows, hidden), jnp.float32),
             pltpu.VMEM((rows, hidden), jnp.float32),
             dma((4,)), dma((4,)), dma, dma((hidden // 128 + 1,)),
@@ -416,7 +417,7 @@
         for n in range(parts):
             at = code * parts + n
             src = p.at[code, 1 - c, :, pl.ds(n * hidden, hidden)]
-            copies[0, code, n] = remote(src, r0.at[pl.ds(at * block, block), :], s0.at[at], q0.at[at], partner)
+            copies[0, code, n] = remote(src, r0.at[pl.ds(at * block, block), pl.ds(0, hidden)], s0.at[at], q0.at[at], partner)
     for k, axes in enumerate(AXES):
         cols = pl.ds(*columns[k])
         for code in range(8):
@@ -460,7 +461,7 @@
             copies[0, code, n].wait_recv()
             cols = pl.ds(n * hidden, hidden)
             mine = p.at[code, c, :, cols]
-            add_into(mine, mine, r0.at[pl.ds((code * parts + n) * block, block), :])
+            add_into(mine, mine, r0.at[pl.ds((code * parts + n) * block, block), pl.ds(0, hidden)])
         for k, axes in enumerate(AXES):
             if (code >> axes[0]) & 1:
                 copies[1, k, slot_one(code, axes)].start()
@@ -490,7 +491,7 @@
     bias_stage(0)
 
     loads[4].wait()
-    step = min(hidden, 512)
+    step = BLK
 
     @pl.loop(0, hidden // step)
     def _(n):
@@ -601,7 +602,7 @@
         pltpu.VMEM((2 * hidden, total), jnp.bfloat16),
         pltpu.VMEM((hidden, width), jnp.bfloat16),
         pltpu.VMEM((8, 2, block, width), jnp.bfloat16),
-        pltpu.VMEM((width, hidden), jnp.bfloat16),
+        pltpu.VMEM((width, hidden + PAD), jnp.bfloat16),
         pltpu.VMEM((4, block, width), jnp.bfloat16),
         pltpu.VMEM((2, block, width), jnp.bfloat16),
         pltpu.VMEM((block, width), jnp.bfloat16),
@@ -650,7 +651,7 @@
 
 def widen(total, part, layer, layers):
     height, width = part.shape
-    block = min(height, 256)
+    block = min(height, 128)
     return pl.pallas_call(
         widen_kernel,
         grid=(height // block,),

time: 734 us -> 734 us (level)
  transfers between devices with their start and end apart: 4 -> 4, of which waited for: 4 -> 4; matrix products, arithmetic and copies ran while one was open for 1% -> 1% of each run, Pallas kernels for 55% -> 56%
where the time goes in v4:
time: 734 us; the launch traced here: 731 us
  Pallas kernels  675 us (92%)
  waiting for transfers between devices  33.5 us (5%)
  between operations  13.8 us (2%)
    pallas_call x4, Pallas kernels, grads(): pl.pallas_call(functools.partial(grads_kernel, layer, rows, hidden), in_s...  434 us
    pallas_call x1, Pallas kernels, forward(): pl.pallas_call(functools.partial(forward_kernel, rows), in_specs=[hbm, hb...  134 us
    pallas_call x4, Pallas kernels, widen(): pl.pallas_call(widen_kernel, grid=(height // block,), in_specs=[pl.BlockS...  75.1 us
    all_gather x4, waiting for transfers between devices, local_grads(): waiting = lax.all_gather(shard, batch_axes, axis=0, tiled=True)  33.4 us
    pallas_call x1, Pallas kernels, backward(): pl.pallas_call(functools.partial(backward_kernel, layer, rows, steps, hid...  31.9 us
  transfers between devices with their start and end apart: 4, of which 4 were waited for; matrix products, arithmetic and copies ran while one was open for 1% of the time, Pallas kernels for 56%

profile of v4, /device:TPU:0, one launch (start us, length us, event | category | flops | bytes accessed | tf_op | source)
XLA Modules:
  0.0 731.4 jit_solution(10179724487384557292)
XLA Ops:
  7.2 0.0 all-gather.5.cloned.1.call-start
  7.2 2.8 copy.10
  10.0 134.3 %lstm_forward.1 = (bf16[4,544,1024]{2,1,0:T(8,128)(2,1)}, f32[4,512,4096]{2,1,0:T(8,128)}, f32[4,544,1024]{2,1,0:T(8,128)}) custom-call(bf16[512,1024]{1,0:T(8,128)(2,1)} %bitcast.10, bf16[4,2048,4096]{2,1,0:T(8,128)(2,1)} %w_hbm.11, f32[4,4096]{1,0:T(4,128)} %b_ref.1), custom_call_target="tpu_custom_call" | custom-call | flops 34359738368 | bytes 75497472 | tf_op jit(solution)/shard_map/lstm_forward/pallas_call | solution.py:164
  144.3 31.9 %lstm_backward_3.1 = (bf16[512,4096]{1,0:T(8,128)(2,1)}, f32[8,4096]{1,0:T(8,128)}) custom-call(f32[512,1024]{1,0:T(8,128)} %bitcast.15, bf16[4,2048,4096]{2,1,0:T(8,128)(2,1)} %w_hbm.11, f32[4,512,4096]{2,1,0:T(8,128)} %get-tuple-element.31.gates_hbm, f32[4,544,1024]{2,1,0:T(8,128)} %get-tuple-element.32.c_hbm), custom_call_target="tpu_custom_call" | custom-call | flops 85899345920 | bytes 23068672 | tf_op jit(solution)/shard_map/lstm_backward_3/pallas_call | solution.py:304
  176.1 82.3 %lstm_grads_3.1 = (bf16[128,4096]{1,0:T(8,128)(2,1)}, f32[1,4096]{1,0:T(1,128)}, bf16[512,4096]{1,0:T(8,128)(2,1)}, f32[8,4096]{1,0:T(8,128)}) custom-call(bf16[512,4096]{1,0:T(8,128)(2,1)} %get-tuple-element.33.dz_hbm, f32[8,4096]{1,0:T(8,128)} %get-tuple-element.34.db_hbm, bf16[512,1024]{1,0:T(8,128)(2,1)} %bitcast.11, ...), custom_call_target="tpu_custom_call" | custom-call | flops 64424509440 | bytes 33554432 | tf_op jit(solution)/shard_map/lstm_grads_3/pallas_call | solution.py:632
  258.4 0.0 all-gather.5.cloned.1.call-update
  258.5 0.2 all-gather.7.cloned.1.call-start
  258.7 117.7 %lstm_grads_2.1 = (bf16[128,4096]{1,0:T(8,128)(2,1)}, f32[1,4096]{1,0:T(1,128)}, bf16[512,4096]{1,0:T(8,128)(2,1)}, f32[8,4096]{1,0:T(8,128)}) custom-call(bf16[512,4096]{1,0:T(8,128)(2,1)} %get-tuple-element.37.dz_hbm, f32[8,4096]{1,0:T(8,128)} %get-tuple-element.38.db_hbm, bf16[512,1024]{1,0:T(8,128)(2,1)} %bitcast.12, ...), custom_call_target="tpu_custom_call" | custom-call | flops 64424509440 | bytes 33554432 | tf_op jit(solution)/shard_map/lstm_grads_2/pallas_call | solution.py:632
  376.4 3.8 all-gather.5.cloned.1.call-done.part_ref
  380.2 0.0 all-gather.7.cloned.1.call-update
  380.2 0.0 all-gather.9.cloned.1.call-start
  380.3 119.7 %lstm_grads_1.1 = (bf16[128,4096]{1,0:T(8,128)(2,1)}, f32[1,4096]{1,0:T(1,128)}, bf16[512,4096]{1,0:T(8,128)(2,1)}, f32[8,4096]{1,0:T(8,128)}) custom-call(bf16[512,4096]{1,0:T(8,128)(2,1)} %get-tuple-element.41.dz_hbm, f32[8,4096]{1,0:T(8,128)} %get-tuple-element.42.db_hbm, bf16[512,1024]{1,0:T(8,128)(2,1)} %bitcast.13, ...), custom_call_target="tpu_custom_call" | custom-call | flops 64424509440 | bytes 33554432 | tf_op jit(solution)/shard_map/lstm_grads_1/pallas_call | solution.py:632
  499.9 5.4 all-gather.7.cloned.1.call-done.part_ref
  505.3 0.0 all-gather.9.cloned.1.call-update
  505.3 0.3 all-gather.11.cloned.1.call-start
  505.6 114.2 %lstm_grads_0.1 = (bf16[128,4096]{1,0:T(8,128)(2,1)}, f32[1,4096]{1,0:T(1,128)}, f32[512,1024]{1,0:T(8,128)}) custom-call(bf16[512,4096]{1,0:T(8,128)(2,1)} %get-tuple-element.45.dz_hbm, f32[8,4096]{1,0:T(8,128)} %get-tuple-element.46.db_hbm, bf16[512,1024]{1,0:T(8,128)(2,1)} %bitcast.14, bf16[4,544,1024]{2,1,0:T(8,128)(2,1)} %get-tuple-element.35.h_hbm, ...), custom_call_target="tpu_custom_call" | custom-call | flops 64424509440 | bytes 33554432 | tf_op jit(solution)/shard_map/lstm_grads_0/pallas_call | solution.py:632
  619.8 7.9 %all-gather.9.cloned.1.call-done.part_ref = bf16[2048,4096]{1,0:T(8,128)(2,1)} async-done(((bf16[128,4096]{1,0:T(8,128)(2,1)}), bf16[2048,4096]{1,0:T(8,128)(2,1)}) %all-gather.9.cloned.1.call-update) | async-done | bytes 16777232 | tf_op jit(solution)/shard_map/all_gather | solution.py:690
  627.7 0.0 all-gather.11.cloned.1.call-update
  627.7 4.1 copy.13
  631.8 1.5 pad_maximum_fusion
  633.3 18.8 %widen_3.1.refs_0_ = f32[4,2048,4096]{2,1,0:T(8,128)} custom-call(bf16[2048,4096]{1,0:T(8,128)(2,1)} %all-gather.5.cloned.1.call-done.part_ref), custom_call_target="tpu_custom_call" | custom-call | flops 8388608 | bytes 50331648 | tf_op jit(solution)/shard_map/widen_3/pallas_call | solution.py:655
  652.1 18.8 %widen_2.1.refs_0_ = f32[4,2048,4096]{2,1,0:T(8,128)} custom-call(bf16[2048,4096]{1,0:T(8,128)(2,1)} %all-gather.7.cloned.1.call-done.part_ref, f32[4,2048,4096]{2,1,0:T(8,128)} %widen_3.1.refs_0_), custom_call_target="tpu_custom_call", output_to_operand_aliasing={{}: (1, {})} | custom-call | flops 8388608 | bytes 50331648 | tf_op jit(solution)/shard_map/widen_2/pallas_call | solution.py:655
  670.8 18.8 %widen_1.1.refs_0_ = f32[4,2048,4096]{2,1,0:T(8,128)} custom-call(bf16[2048,4096]{1,0:T(8,128)(2,1)} %all-gather.9.cloned.1.call-done.part_ref, f32[4,2048,4096]{2,1,0:T(8,128)} %widen_2.1.refs_0_), custom_call_target="tpu_custom_call", output_to_operand_aliasing={{}: (1, {})} | custom-call | flops 8388608 | bytes 50331648 | tf_op jit(solution)/shard_map/widen_1/pallas_call | solution.py:655
  689.6 16.4 %all-gather.11.cloned.1.call-done.part_ref = bf16[2048,4096]{1,0:T(8,128)(2,1)} async-done(((bf16[128,4096]{1,0:T(8,128)(2,1)}), bf16[2048,4096]{1,0:T(8,128)(2,1)}) %all-gather.11.cloned.1.call-update) | async-done | bytes 16777232 | tf_op jit(solution)/shard_map/all_gather | solution.py:690
  706.1 18.8 %widen_0.1 = f32[4,2048,4096]{2,1,0:T(8,128)} custom-call(bf16[2048,4096]{1,0:T(8,128)(2,1)} %all-gather.11.cloned.1.call-done.part_ref, f32[4,2048,4096]{2,1,0:T(8,128)} %widen_1.1.refs_0_), custom_call_target="tpu_custom_call", output_to_operand_aliasing={{}: (1, {})} | custom-call | flops 8388608 | bytes 50331648 | tf_op jit(solution)/shard_map/widen_0/pallas_call | solution.py:655
Async XLA Ops:
  7.2 373.0 %all-gather.5.cloned.1.call-start = ((), (), s32[]{:S(2)}) async-start(), calls=%async_computation | async-start | bytes 17825792 | tf_op jit(solution)/shard_map/all_gather | solution.py:690
  258.5 246.8 %all-gather.7.cloned.1.call-start = ((), (), s32[]{:S(2)}) async-start(), calls=%async_computation.1 | async-start | bytes 17825792 | tf_op jit(solution)/shard_map/all_gather | solution.py:690
  380.2 247.5 %all-gather.9.cloned.1.call-start = ((), (), s32[]{:S(2)}) async-start(), calls=%async_computation.2 | async-start | bytes 17825792 | tf_op jit(solution)/shard_map/all_gather | solution.py:690
  505.3 200.7 %all-gather.11.cloned.1.call-start = ((), (), s32[]{:S(2)}) async-start(), calls=%async_computation.3 | async-start | bytes 17825792 | tf_op jit(solution)/shard_map/all_gather | solution.py:690
Sparse Core Ops, SparseCore 0:
  258.6 121.5 all-gather.4
  382.4 122.7 all-gather.6
  507.5 120.0 all-gather.8
  629.8 76.2 all-gather.10

commit v5 on v4

--- a/solution.py
+++ b/solution.py
@@ -651,7 +651,7 @@
 
 def widen(total, part, layer, layers):
     height, width = part.shape
-    block = min(height, 128)
+    block = min(height, 256)
     return pl.pallas_call(
         widen_kernel,
         grid=(height // block,),
@@ -676,22 +676,23 @@
         e_rows = dy_loc.reshape(rows * steps, hidden)
         h_all, gates, c_all = forward(x_rows, w_stack, b_stack, rows)
         db_list = []
-        dw_sum = None
-        waiting = None
+        gathered = []
         dz, db = backward(layers - 1, e_rows, w_stack, gates, c_all, rows)
         for layer in reversed(range(layers)):
             shard, db_sum, *rest = grads(layer, dz, db, x_rows, h_all, w_stack, gates, c_all, rows)
             if layer:
                 dz, db = rest
             db_list.append(db_sum)
-            if waiting is not None:
-                summed, shard = lax.optimization_barrier((waiting, shard))
-                dw_sum = widen(dw_sum, summed, layer + 1, layers)
-            waiting = lax.all_gather(shard, batch_axes, axis=0, tiled=True)
+            gathered.append((layer, lax.all_gather(shard, batch_axes, axis=0, tiled=True)))
         e_rows = rest[0]
         db_sum = jnp.concatenate(db_list[::-1], axis=0)
-        waiting, dw_sum = lax.optimization_barrier((waiting, dw_sum))
-        dw_sum = widen(dw_sum, waiting, 0, layers)
+        dw_sum = None
+        for layer, summed in gathered:
+            if dw_sum is None:
+                summed, e_rows = lax.optimization_barrier((summed, e_rows))
+            else:
+                summed, dw_sum = lax.optimization_barrier((summed, dw_sum))
+            dw_sum = widen(dw_sum, summed, layer, layers)
         dx = jnp.swapaxes(e_rows.reshape(steps, rows, hidden), 0, 1)
         return dw_sum, db_sum, dx
 

time: 734 us -> 718 us (0.978)
  Pallas kernels: 675 us -> 652 us
  waiting for transfers between devices: 33.5 us -> 44.6 us
    pallas_call x4, Pallas kernels: 434 us -> 412 us  [grads(): pl.pallas_call(functools.partial(grads_kernel, layer, rows, hidden), in_s...]
    all_gather x4, waiting for transfers between devices: 33.4 us -> 44.6 us  [local_grads(): lax.all_gather(shard, batch_axes, axis=0, tiled=True)]
  transfers between devices with their start and end apart: 4 -> 4, of which waited for: 4 -> 1; matrix products, arithmetic and copies ran while one was open for 1% -> 0% of each run, Pallas kernels for 56% -> 54%
where the time goes in v5:
time: 718 us
  Pallas kernels  652 us (91%)
  waiting for transfers between devices  44.6 us (6%)
  between operations  13.8 us (2%)
    pallas_call x4, Pallas kernels, grads(): pl.pallas_call(functools.partial(grads_kernel, layer, rows, hidden), in_s...  412 us
    pallas_call x1, Pallas kernels, forward(): pl.pallas_call(functools.partial(forward_kernel, rows), in_specs=[hbm, hb...  134 us
    pallas_call x4, Pallas kernels, widen(): pl.pallas_call(widen_kernel, grid=(height // block,), in_specs=[pl.BlockS...  73.3 us
    all_gather x4, waiting for transfers between devices, local_grads(): lax.all_gather(shard, batch_axes, axis=0, tiled=True)  44.6 us
    pallas_call x1, Pallas kernels, backward(): pl.pallas_call(functools.partial(backward_kernel, layer, rows, steps, hid...  31.9 us
  transfers between devices with their start and end apart: 4, of which 1 were waited for; matrix products, arithmetic and copies ran while one was open for 0% of the time, Pallas kernels for 54%

profile of v5, /device:TPU:0, one launch (start us, length us, event | category | flops | bytes accessed | tf_op | source)
XLA Modules:
  0.0 717.5 jit_solution(3799662764674683126)
XLA Ops:
  7.2 0.0 all-gather.11.cloned.1.call-start
  7.2 2.8 copy.10
  10.0 134.3 %lstm_forward.1 = (bf16[4,544,1024]{2,1,0:T(8,128)(2,1)}, f32[4,512,4096]{2,1,0:T(8,128)}, f32[4,544,1024]{2,1,0:T(8,128)}) custom-call(bf16[512,1024]{1,0:T(8,128)(2,1)} %bitcast.10, bf16[4,2048,4096]{2,1,0:T(8,128)(2,1)} %w_hbm.11, f32[4,4096]{1,0:T(4,128)} %b_ref.1), custom_call_target="tpu_custom_call" | custom-call | flops 34359738368 | bytes 75497472 | tf_op jit(solution)/shard_map/lstm_forward/pallas_call | solution.py:164
  144.3 31.9 %lstm_backward_3.1 = (bf16[512,4096]{1,0:T(8,128)(2,1)}, f32[8,4096]{1,0:T(8,128)}) custom-call(f32[512,1024]{1,0:T(8,128)} %bitcast.15, bf16[4,2048,4096]{2,1,0:T(8,128)(2,1)} %w_hbm.11, f32[4,512,4096]{2,1,0:T(8,128)} %get-tuple-element.31.gates_hbm, f32[4,544,1024]{2,1,0:T(8,128)} %get-tuple-element.32.c_hbm), custom_call_target="tpu_custom_call" | custom-call | flops 85899345920 | bytes 23068672 | tf_op jit(solution)/shard_map/lstm_backward_3/pallas_call | solution.py:304
  176.1 82.3 %lstm_grads_3.1 = (bf16[128,4096]{1,0:T(8,128)(2,1)}, f32[1,4096]{1,0:T(1,128)}, bf16[512,4096]{1,0:T(8,128)(2,1)}, f32[8,4096]{1,0:T(8,128)}) custom-call(bf16[512,4096]{1,0:T(8,128)(2,1)} %get-tuple-element.33.dz_hbm, f32[8,4096]{1,0:T(8,128)} %get-tuple-element.34.db_hbm, bf16[512,1024]{1,0:T(8,128)(2,1)} %bitcast.11, ...), custom_call_target="tpu_custom_call" | custom-call | flops 64424509440 | bytes 33554432 | tf_op jit(solution)/shard_map/lstm_grads_3/pallas_call | solution.py:632
  258.5 0.0 all-gather.11.cloned.1.call-update
  258.5 0.2 all-gather.9.cloned.1.call-start
  258.7 117.7 %lstm_grads_2.1 = (bf16[128,4096]{1,0:T(8,128)(2,1)}, f32[1,4096]{1,0:T(1,128)}, bf16[512,4096]{1,0:T(8,128)(2,1)}, f32[8,4096]{1,0:T(8,128)}) custom-call(bf16[512,4096]{1,0:T(8,128)(2,1)} %get-tuple-element.36.dz_hbm, f32[8,4096]{1,0:T(8,128)} %get-tuple-element.37.db_hbm, bf16[512,1024]{1,0:T(8,128)(2,1)} %bitcast.12, ...), custom_call_target="tpu_custom_call" | custom-call | flops 64424509440 | bytes 33554432 | tf_op jit(solution)/shard_map/lstm_grads_2/pallas_call | solution.py:632
  376.4 0.0 all-gather.9.cloned.1.call-update
  376.5 0.0 all-gather.7.cloned.1.call-start
  376.5 113.7 %lstm_grads_1.1 = (bf16[128,4096]{1,0:T(8,128)(2,1)}, f32[1,4096]{1,0:T(1,128)}, bf16[512,4096]{1,0:T(8,128)(2,1)}, f32[8,4096]{1,0:T(8,128)}) custom-call(bf16[512,4096]{1,0:T(8,128)(2,1)} %get-tuple-element.38.dz_hbm, f32[8,4096]{1,0:T(8,128)} %get-tuple-element.39.db_hbm, bf16[512,1024]{1,0:T(8,128)(2,1)} %bitcast.13, ...), custom_call_target="tpu_custom_call" | custom-call | flops 64424509440 | bytes 33554432 | tf_op jit(solution)/shard_map/lstm_grads_1/pallas_call | solution.py:632
  490.2 0.0 all-gather.7.cloned.1.call-update
  490.2 0.3 all-gather.5.cloned.1.call-start
  490.5 98.5 %lstm_grads_0.1 = (bf16[128,4096]{1,0:T(8,128)(2,1)}, f32[1,4096]{1,0:T(1,128)}, f32[512,1024]{1,0:T(8,128)}) custom-call(bf16[512,4096]{1,0:T(8,128)(2,1)} %get-tuple-element.40.dz_hbm, f32[8,4096]{1,0:T(8,128)} %get-tuple-element.41.db_hbm, bf16[512,1024]{1,0:T(8,128)(2,1)} %bitcast.14, bf16[4,544,1024]{2,1,0:T(8,128)(2,1)} %get-tuple-element.35.h_hbm, ...), custom_call_target="tpu_custom_call" | custom-call | flops 64424509440 | bytes 33554432 | tf_op jit(solution)/shard_map/lstm_grads_0/pallas_call | solution.py:632
  589.1 0.0 all-gather.5.cloned.1.call-update
  589.1 1.5 pad_maximum_fusion
  590.6 0.0 all-gather.11.cloned.1.call-done.part_ref
  590.6 18.3 %widen_3.1.refs_0_ = f32[4,2048,4096]{2,1,0:T(8,128)} custom-call(bf16[2048,4096]{1,0:T(8,128)(2,1)} %all-gather.11.cloned.1.call-done.part_ref), custom_call_target="tpu_custom_call" | custom-call | flops 8388608 | bytes 50331648 | tf_op jit(solution)/shard_map/widen_3/pallas_call | solution.py:655
  608.8 0.0 all-gather.9.cloned.1.call-done.part_ref
  608.8 18.3 %widen_2.1.refs_0_ = f32[4,2048,4096]{2,1,0:T(8,128)} custom-call(bf16[2048,4096]{1,0:T(8,128)(2,1)} %all-gather.9.cloned.1.call-done.part_ref, f32[4,2048,4096]{2,1,0:T(8,128)} %widen_3.1.refs_0_), custom_call_target="tpu_custom_call", output_to_operand_aliasing={{}: (1, {})} | custom-call | flops 8388608 | bytes 50331648 | tf_op jit(solution)/shard_map/widen_2/pallas_call | solution.py:655
  627.1 0.0 copy-start
  627.1 0.0 all-gather.7.cloned.1.call-done.part_ref
  627.1 18.4 %widen_1.1.refs_0_ = f32[4,2048,4096]{2,1,0:T(8,128)} custom-call(bf16[2048,4096]{1,0:T(8,128)(2,1)} %all-gather.7.cloned.1.call-done.part_ref, f32[4,2048,4096]{2,1,0:T(8,128)} %widen_2.1.refs_0_), custom_call_target="tpu_custom_call", output_to_operand_aliasing={{}: (1, {})} | custom-call | flops 8388608 | bytes 50331648 | tf_op jit(solution)/shard_map/widen_1/pallas_call | solution.py:655
  645.6 44.6 %all-gather.5.cloned.1.call-done.part_ref = bf16[2048,4096]{1,0:T(8,128)(2,1)} async-done(((bf16[128,4096]{1,0:T(8,128)(2,1)}), bf16[2048,4096]{1,0:T(8,128)(2,1)}) %all-gather.5.cloned.1.call-update) | async-done | bytes 16777232 | tf_op jit(solution)/shard_map/all_gather | solution.py:686
  690.1 0.0 copy-done
  690.1 2.5 copy.13
  692.7 18.3 %widen_0.1 = f32[4,2048,4096]{2,1,0:T(8,128)} custom-call(bf16[2048,4096]{1,0:T(8,128)(2,1)} %all-gather.5.cloned.1.call-done.part_ref, f32[4,2048,4096]{2,1,0:T(8,128)} %widen_1.1.refs_0_), custom_call_target="tpu_custom_call", output_to_operand_aliasing={{}: (1, {})} | custom-call | flops 8388608 | bytes 50331648 | tf_op jit(solution)/shard_map/widen_0/pallas_call | solution.py:655
Async XLA Ops:
  7.2 583.4 %all-gather.11.cloned.1.call-start = ((), (), s32[]{:S(2)}) async-start(), calls=%async_computation.3 | async-start | bytes 17825792 | tf_op jit(solution)/shard_map/all_gather | solution.py:686
  258.5 350.4 %all-gather.9.cloned.1.call-start = ((), (), s32[]{:S(2)}) async-start(), calls=%async_computation.2 | async-start | bytes 17825792 | tf_op jit(solution)/shard_map/all_gather | solution.py:686
  376.5 250.7 %all-gather.7.cloned.1.call-start = ((), (), s32[]{:S(2)}) async-start(), calls=%async_computation.1 | async-start | bytes 17825792 | tf_op jit(solution)/shard_map/all_gather | solution.py:686
  490.2 199.9 %all-gather.5.cloned.1.call-start = ((), (), s32[]{:S(2)}) async-start(), calls=%async_computation | async-start | bytes 17825792 | tf_op jit(solution)/shard_map/all_gather | solution.py:686
  627.1 63.0 %copy-start = (f32[512,1024]{1,0:T(8,128)S(1)}, f32[512,1024]{1,0:T(8,128)}, u32[]{:S(2)}) copy-start(f32[512,1024]{1,0:T(8,128)} %get-tuple-element.58) | copy-start | bytes 6291460
Sparse Core Ops, SparseCore 0:
  258.6 121.5 all-gather.10
  382.5 117.1 all-gather.8
  501.9 108.5 all-gather.6
  612.6 77.5 all-gather.4
